TPU v7x, 1024 devices: a whole 8x8x8 slice. The times are simulated.
1024 devices in a mesh: group: 16 (over y, core), dev: 64 (over z, x).
Axes of the slice: x: 8, y: 8, z: 8, core: 2. Of those that a mesh axis runs over, the one named last changes fastest.
Arguments:
- solution: float32 [16, 128, 16, 512], P('group', 'dev'), may hold values from -6 to 6
- residual: float32 [16, 128, 16, 512], P('group', 'dev'), may hold values from -6 to 6
- direction: float32 [16, 128, 16, 512], P('group', 'dev'), may hold values from -0.03 to 0.03
- geometry: bfloat16 [3, 16, 128, 16, 512], P(None, 'group', 'dev'), may hold values from 0.5 to 2
- mass: bfloat16 [16, 128, 16, 512], P('group', 'dev'), may hold values from 50 to 500
Outputs:
- solution_out: float32 [16, 128, 16, 512], P('group', 'dev')
- residual_out: float32 [16, 128, 16, 512], P('group', 'dev')
- direction_out: float32 [16, 128, 16, 512], P('group', 'dev')
All inputs are finite; a program needn't handle non-finite values.
Results may differ from a plain program's by a relative error of at most 0.0003.
Values sent between devices are 32-bit elements; how exact they have to be, the bound alone decides.
No kernel may reach another device: no remote copies, remote signals or barrier semaphores. Data moves between devices by JAX's collectives and lax.ppermute only.
A program may use at most 32 MiB of HBM per device.

v0:
```python
import jax
import jax.numpy as jnp
import numpy as np
from jax import lax
from jax.sharding import Mesh
from jax.sharding import PartitionSpec as P

NP = 8
GROUP = ("group_0", "group_1")
DEV = ("dev_0", "dev_1")
GROUP_DEV = ("group_0", "group_1", "dev_0", "dev_1")


lobatto_nodes = [
    -1.0,
    -0.8717401485096066,
    -0.5917001814331423,
    -0.2092992179024789,
    0.2092992179024789,
    0.5917001814331423,
    0.8717401485096066,
    1.0,
]


def extended(value, sides, width):
    for axis, dim in sides:
        peers, length = (lax.axis_size(axis), value.shape[dim])
        up = [(i, (i + 1) % peers) for i in range(peers)]
        down = [(j, i) for i, j in up]
        last = lax.slice_in_dim(value, length - width, length, axis=dim)
        initial = lax.slice_in_dim(value, 0, width, axis=dim)
        before = lax.ppermute(last, axis, up)
        after = lax.ppermute(initial, axis, down)
        value = jnp.concatenate([before, value, after], axis=dim)
    return value


def by_axis(value, axes):
    for axis in axes:
        value = lax.psum(value, axis)
    return value


def derivative_table():
    nodes = np.array(lobatto_nodes)
    identity = np.eye(NP)
    offset = nodes[:, None] - nodes[None, :] + identity
    barycentric = 1.0 / np.prod(offset, axis=1)
    derivative = barycentric[None, :] / barycentric[:, None] / offset * (1.0 - identity)
    return derivative - identity * np.sum(derivative, axis=1)[:, None]


def operator_tables():
    derivative = derivative_table()
    identity = np.eye(NP)
    kron_list = [
        np.kron(np.kron(derivative, identity), identity),
        np.kron(np.kron(identity, derivative), identity),
        np.kron(np.kron(identity, identity), derivative),
    ]
    forward = np.concatenate([matrix.T for matrix in kron_list], axis=1)
    backward = np.concatenate(kron_list, axis=0)
    squares = np.concatenate([matrix * matrix for matrix in kron_list], axis=0)
    return (
        jnp.asarray(forward, dtype=jnp.float32),
        jnp.asarray(backward, dtype=jnp.float32),
        jnp.asarray(squares, dtype=jnp.float32),
    )


def point_weights():
    edge = np.where(np.arange(NP) % (NP - 1) == 0, 0.5, 1.0)
    return jnp.asarray(np.kron(np.kron(edge, edge), edge), dtype=jnp.float32)


def highest(left, right):
    return jnp.dot(left, right, precision=lax.Precision.HIGHEST, preferred_element_type=jnp.float32)


def combine_faces(field, lower, upper, prev_upper, next_lower, elem_dim, node_dim):
    extent = field.shape[elem_dim]
    lower_next = jnp.concatenate(
        [lax.slice_in_dim(lower, 1, extent, axis=elem_dim), next_lower], axis=elem_dim
    )
    summed = upper + lower_next
    leading = prev_upper + lax.slice_in_dim(lower, 0, 1, axis=elem_dim)
    new_lower = jnp.concatenate(
        [leading, lax.slice_in_dim(summed, 0, extent - 1, axis=elem_dim)], axis=elem_dim
    )
    middle = lax.slice_in_dim(field, 1, NP - 1, axis=node_dim)
    return jnp.concatenate([new_lower, middle, summed], axis=node_dim)


def local_pass(field, elem_dim, node_dim, prev_upper, next_lower):
    lower = lax.index_in_dim(field, 0, node_dim, keepdims=True)
    upper = lax.index_in_dim(field, NP - 1, node_dim, keepdims=True)
    return combine_faces(field, lower, upper, prev_upper, next_lower, elem_dim, node_dim)


def group_pass(field):
    lower = lax.index_in_dim(field, 0, 4, keepdims=True)
    upper = lax.index_in_dim(field, NP - 1, 4, keepdims=True)
    extent = field.shape[1]
    end_faces = jnp.concatenate(
        [
            lax.slice_in_dim(lower, 0, 1, axis=1),
            lax.slice_in_dim(upper, extent - 1, extent, axis=1),
        ],
        axis=1,
    )
    padded = extended(end_faces, ((GROUP, 1),), 1)
    return combine_faces(field, lower, upper, padded[:, 0:1], padded[:, 3:4], 1, 4)


def dev_neighbours(field):
    lower = lax.index_in_dim(field, 0, 5, keepdims=True)
    upper = lax.index_in_dim(field, NP - 1, 5, keepdims=True)
    extent = field.shape[2]
    end_faces = jnp.concatenate(
        [
            lax.slice_in_dim(lower, 0, 1, axis=2),
            lax.slice_in_dim(upper, extent - 1, extent, axis=2),
        ],
        axis=2,
    )
    padded = extended(end_faces, ((DEV, 2),), 1)
    return (padded[:, :, 0:1], padded[:, :, 3:4])


def dev_pass(field):
    before, after = dev_neighbours(field)
    return local_pass(field, 2, 5, before, after)


def assemble(stacked):
    shaped = stacked.reshape(stacked.shape[:4] + (NP, NP, NP))
    shaped = group_pass(dev_pass(shaped))
    extent = shaped.shape[3]
    lower = lax.index_in_dim(shaped, 0, 6, keepdims=True)
    upper = lax.index_in_dim(shaped, NP - 1, 6, keepdims=True)
    shaped = combine_faces(
        shaped,
        lower,
        upper,
        lax.slice_in_dim(upper, extent - 1, extent, axis=3),
        lax.slice_in_dim(lower, 0, 1, axis=3),
        3,
        6,
    )
    return shaped.reshape(stacked.shape)


def on_device(solution, residual, direction, geometry, mass):
    forward, backward, squares = operator_tables()
    weights = point_weights()
    points = NP**3
    dims_full = solution.shape
    elements = dims_full[0] * dims_full[1] * dims_full[2]
    geometry_rows = jnp.moveaxis(geometry.astype(jnp.float32), 0, -2).reshape(elements, 3 * points)
    mass_coef = mass.astype(jnp.float32).reshape(elements, points)
    diag_local = (highest(geometry_rows, squares) + mass_coef).reshape(dims_full)
    both = assemble(jnp.stack([diag_local, weights * direction]))
    diagonal = both[0]
    smooth = both[1]
    flat = smooth.reshape(elements, points)
    fluxes = geometry_rows * highest(flat, forward)
    applied_local = highest(fluxes, backward) + mass_coef * flat
    applied = assemble(applied_local.reshape((1,) + dims_full))[0]
    scaled = residual / diagonal
    norm_now, curvature, cross_term, quad_term = (
        by_axis(jnp.sum(weights * residual * scaled), GROUP_DEV),
        by_axis(jnp.sum(weights * smooth * applied), GROUP_DEV),
        by_axis(jnp.sum(weights * scaled * applied), GROUP_DEV),
        by_axis(jnp.sum(weights * applied * applied / diagonal), GROUP_DEV),
    )
    step_size = norm_now / curvature
    residual_out = residual - step_size * applied
    norm_next = norm_now - 2.0 * step_size * cross_term + step_size * step_size * quad_term
    solution_out = solution + step_size * smooth
    direction_out = residual_out / diagonal + norm_next / norm_now * smooth
    return (solution_out, residual_out, direction_out)


def solution(mesh):
    finer = Mesh(mesh.devices.reshape(8, 2, 8, 8), ("group_0", "group_1", "dev_0", "dev_1"))
    return jax.shard_map(
        on_device,
        mesh=finer,
        in_specs=(
            P(GROUP, DEV, None, None),
            P(GROUP, DEV, None, None),
            P(GROUP, DEV, None, None),
            P(None, GROUP, DEV, None, None),
            P(GROUP, DEV, None, None),
        ),
        out_specs=(P(GROUP, DEV, None, None), P(GROUP, DEV, None, None), P(GROUP, DEV, None, None)),
        check_vma=False,
    )
```

profile of v0, /device:TPU:18, one launch (start us, length us, event | category | flops | bytes accessed | tf_op | source)
XLA Modules:
  0.0 133.7 jit_solution(6763835682005487921)
XLA Ops:
  0.6 0.0 copy-start.5
  0.6 1.0 copy.31
  1.7 0.0 copy-start.8
  1.7 3.1 %fusion = f32[32,512]{1,0:T(8,128)S(1)} fusion(f32[1536,512]{1,0:T(8,128)} %constant.14.clone, bf16[32,1536]{1,0:T(8,128)(2,1)S(1)} %bitcast.43, bf16[32,512]{1,0:T(8,128)(2,1)} %bitcast.47), kind=kOutput, calls=%fused_computation.7 | convolution fusion | flops 302022656 | bytes 3342336 | tf_op jit(solution)/shard_map/dot_general | solution.py:78
  4.8 0.1 copy.32
  4.9 0.3 stack.8
  5.3 0.2 copy.33
  5.5 0.1 broadcast_multiply_fusion.2
  5.7 3.4 %collective-permute-start = (f32[2,1,1,16,8,1,8]{3,6,5,4,2,1,0:T(8,128)S(1)}, f32[2,1,1,16,8,1,8]{3,6,5,4,2,1,0:T(8,128)S(1)}, u32[]{:S(2)}, u32[]{:S(2)}) collective-permute-start(f32[2,1,1,16,8,1,8]{3,6,5,4,2,1,0:T(8,128)S(1)} %pad_maximum_fusion.8), channel_id=1, source_target_pairs={{0,1},{1,2},{2,3},{3,4},{4,5},{5,6},{6,7},{7,8},{8,9},{9,10},{10,1... | collective-permute-start | bytes 24584 | tf_op jit(solution)/shard_map/ppermute | solution.py:33
  9.1 2.8 %collective-permute-done = f32[2,1,1,16,8,1,8]{3,6,5,4,2,1,0:T(8,128)S(1)} collective-permute-done((f32[2,1,1,16,8,1,8]{3,6,5,4,2,1,0:T(8,128)S(1)}, f32[2,1,1,16,8,1,8]{3,6,5,4,2,1,0:T(8,128)S(1)}, u32[]{:S(2)}, u32[]{:S(2)}) %collective-permute-start) | collective-permute-done | bytes 8224 | tf_op jit(solution)/shard_map/ppermute | solution.py:33
  11.9 18.1 %collective-permute-start.1 = (f32[2,1,1,16,8,1,8]{3,6,5,4,2,1,0:T(8,128)S(1)}, f32[2,1,1,16,8,1,8]{3,6,5,4,2,1,0:T(8,128)S(1)}, u32[]{:S(2)}, u32[]{:S(2)}) collective-permute-start(f32[2,1,1,16,8,1,8]{3,6,5,4,2,1,0:T(8,128)S(1)} %get-tuple-element.35), channel_id=1, source_target_pairs={{1,0},{2,1},{3,2},{4,3},{5,4},{6,5},{7,6},{8,7},{9,8},{10,9},{11,1... | collective-permute-start | bytes 24584 | tf_op jit(solution)/shard_map/ppermute | solution.py:34
  30.0 1.9 %collective-permute-done.1 = f32[2,1,1,16,8,1,8]{3,6,5,4,2,1,0:T(8,128)S(1)} collective-permute-done((f32[2,1,1,16,8,1,8]{3,6,5,4,2,1,0:T(8,128)S(1)}, f32[2,1,1,16,8,1,8]{3,6,5,4,2,1,0:T(8,128)S(1)}, u32[]{:S(2)}, u32[]{:S(2)}) %collective-permute-start.1) | collective-permute-done | bytes 8224 | tf_op jit(solution)/shard_map/ppermute | solution.py:34
  31.9 0.1 fusion.4
  32.1 0.0 collective-permute-start.2
  32.1 1.7 %collective-permute-start.3 = (f32[2,1,2,16,1,8,8]{3,6,5,4,2,1,0:T(8,128)S(1)}, f32[2,1,2,16,1,8,8]{3,6,5,4,2,1,0:T(8,128)S(1)}, u32[]{:S(2)}, u32[]{:S(2)}) collective-permute-start(f32[2,1,2,16,1,8,8]{3,6,5,4,2,1,0:T(8,128)S(1)} %get-tuple-element.44), channel_id=1, source_target_pairs={{64,0},{128,64},{192,128},{256,192},{320,256},{384,320},{448,384},... | collective-permute-start | bytes 49160 | tf_op jit(solution)/shard_map/ppermute | solution.py:34
  33.9 0.1 slice.157
  33.9 2.6 %collective-permute-done.2 = f32[2,1,2,16,1,8,8]{3,6,5,4,2,1,0:T(8,128)S(1)} collective-permute-done((f32[2,1,2,16,1,8,8]{3,6,5,4,2,1,0:T(8,128)S(1)}, f32[2,1,2,16,1,8,8]{3,6,5,4,2,1,0:T(8,128)S(1)}, u32[]{:S(2)}, u32[]{:S(2)}) %collective-permute-start.2) | collective-permute-done | bytes 16416 | tf_op jit(solution)/shard_map/ppermute | solution.py:33
  36.5 0.0 collective-permute-done.3
  36.5 0.4 maximum_add_fusion
  36.9 0.6 fusion.13
  37.5 0.5 fusion.2
  38.1 0.0 copy-start.4
  38.1 0.4 copy.37
  38.5 0.3 reshape_squeeze.3
  38.8 0.1 copy.38
  38.9 3.9 %convolution_multiply_fusion = f32[32,1536]{1,0:T(8,128)S(1)} fusion(f32[32,512]{0,1:T(8,128)S(1)} %reshape_squeeze.3, f32[512,1536]{1,0:T(8,128)} %constant.12.clone, bf16[32,1536]{1,0:T(8,128)(2,1)S(1)} %bitcast.44), kind=kOutput, calls=%fused_computation | convolution fusion | flops 302088192 | bytes 3506176 | tf_op jit(solution)/shard_map/dot_general | solution.py:78
  42.9 0.0 copy-done.4
  42.9 0.0 copy-done
  42.9 1.9 %convolution_add_fusion = f32[32,512]{1,0:T(8,128)S(1)} fusion(f32[32,1536]{1,0:T(8,128)S(1)} %convolution_multiply_fusion, f32[1536,512]{1,0:T(8,128)S(1)} %copy-done, f32[32,512]{1,0:T(8,128)S(1)} %copy.38, bf16[32,512]{1,0:T(8,128)(2,1)S(1)} %bitcast.48), kind=kOutput, calls=%fused_computation.5 | convolution fusion | flops 302039040 | bytes 3506176 | tf_op jit(solution)/shard_map/dot_general | solution.py:78
  44.8 0.0 copy-start.3
  44.8 0.0 copy-start.6
  44.8 0.1 copy.39
  45.0 0.3 reshape_reshape.3
  45.3 0.1 fusion.19
  45.4 4.3 %collective-permute-start.5 = (f32[1,1,1,16,8,1,8]{3,6,5,4,2,1,0:T(8,128)S(1)}, f32[1,1,1,16,8,1,8]{3,6,5,4,2,1,0:T(8,128)S(1)}, u32[]{:S(2)}, u32[]{:S(2)}) collective-permute-start(f32[1,1,1,16,8,1,8]{3,6,5,4,2,1,0:T(8,128)S(1)} %bitcast.49), channel_id=1, source_target_pairs={{1,0},{2,1},{3,2},{4,3},{5,4},{6,5},{7,6},{8,7},{9,8},{10,9},{11,1... | collective-permute-start | bytes 12296 | tf_op jit(solution)/shard_map/ppermute | solution.py:34
  49.7 1.9 %collective-permute-start.4 = (f32[1,1,1,16,8,1,8]{3,6,5,4,2,1,0:T(8,128)S(1)}, f32[1,1,1,16,8,1,8]{3,6,5,4,2,1,0:T(8,128)S(1)}, u32[]{:S(2)}, u32[]{:S(2)}) collective-permute-start(f32[1,1,1,16,8,1,8]{3,6,5,4,2,1,0:T(8,128)S(1)} %bitcast.53), channel_id=1, source_target_pairs={{0,1},{1,2},{2,3},{3,4},{4,5},{5,6},{6,7},{7,8},{8,9},{9,10},{10,1... | collective-permute-start | bytes 12296 | tf_op jit(solution)/shard_map/ppermute | solution.py:33
  51.7 0.0 collective-permute-done.5
  51.7 7.1 %collective-permute-done.4 = f32[1,1,1,16,8,1,8]{3,6,5,4,2,1,0:T(8,128)S(1)} collective-permute-done((f32[1,1,1,16,8,1,8]{3,6,5,4,2,1,0:T(8,128)S(1)}, f32[1,1,1,16,8,1,8]{3,6,5,4,2,1,0:T(8,128)S(1)}, u32[]{:S(2)}, u32[]{:S(2)}) %collective-permute-start.4) | collective-permute-done | bytes 4128 | tf_op jit(solution)/shard_map/ppermute | solution.py:33
  58.9 0.7 collective-permute-start.6
  59.5 3.0 %collective-permute-done.6 = f32[1,1,2,16,1,8,8]{3,6,5,4,2,1,0:T(8,128)S(1)} collective-permute-done((f32[1,1,2,16,1,8,8]{3,6,5,4,2,1,0:T(8,128)S(1)}, f32[1,1,2,16,1,8,8]{3,6,5,4,2,1,0:T(8,128)S(1)}, u32[]{:S(2)}, u32[]{:S(2)}) %collective-permute-start.6) | collective-permute-done | bytes 8224 | tf_op jit(solution)/shard_map/ppermute | solution.py:33
  62.6 0.0 collective-permute-start.7
  62.6 0.0 copy-done.3
  62.6 0.2 copy.35
  62.8 1.0 copy.36
  63.9 0.2 copy.45
  64.1 0.4 collective-permute-done.7
  64.6 0.1 slice.172
  64.6 0.2 slice_add_fusion.1
  64.9 0.2 slice.170
  65.1 0.2 slice_add_fusion
  65.3 1.1 fusion.10
  66.3 0.0 copy-done.1
  66.3 0.9 multiply_reduce_fusion
  67.2 19.1 %all-reduce.2 = (f32[]{:T(128)}, f32[]{:T(128)}, f32[]{:T(128)}, f32[]{:T(128)}) all-reduce(f32[]{:T(128)} %get-tuple-element.12, f32[]{:T(128)} %get-tuple-element.10, f32[]{:T(128)} %get-tuple-element.11, f32[]{:T(128)} %get-tuple-element.9), channel_id=1, replica_groups=mesh['group_0'=8,'group_1'=2,'dev_0'=8,'dev_1'=8] {'group_0'}, use_global_device_ids=true, to_apply=%region_1.0 | all-reduce | flops 4 | bytes 32 | tf_op jit(solution)/shard_map/psum | solution.py:41
  86.3 3.1 %all-reduce.3 = (f32[]{:T(128)}, f32[]{:T(128)}, f32[]{:T(128)}, f32[]{:T(128)}) all-reduce(f32[]{:T(128)} %get-tuple-element.21, f32[]{:T(128)} %get-tuple-element.22, f32[]{:T(128)} %get-tuple-element.23, f32[]{:T(128)} %get-tuple-element.24), channel_id=1, replica_groups=mesh['group_0'=8,'group_1'=2,'dev_0'=8,'dev_1'=8] {'group_1'}, use_global_device_ids=true, to_apply=%region_2.0 | all-reduce | flops 4 | bytes 32 | tf_op jit(solution)/shard_map/psum | solution.py:41
  89.4 14.8 %all-reduce.1 = (f32[]{:T(128)}, f32[]{:T(128)}, f32[]{:T(128)}, f32[]{:T(128)}) all-reduce(f32[]{:T(128)} %get-tuple-element.25, f32[]{:T(128)} %get-tuple-element.26, f32[]{:T(128)} %get-tuple-element.27, f32[]{:T(128)} %get-tuple-element.28), channel_id=1, replica_groups=mesh['group_0'=8,'group_1'=2,'dev_0'=8,'dev_1'=8] {'dev_0'}, use_global_device_ids=true, to_apply=%region_3.0 | all-reduce | flops 4 | bytes 32 | tf_op jit(solution)/shard_map/psum | solution.py:41
  104.3 20.1 %all-reduce = (f32[]{:T(128)}, f32[]{:T(128)}, f32[]{:T(128)}, f32[]{:T(128)}) all-reduce(f32[]{:T(128)} %get-tuple-element.17, f32[]{:T(128)} %get-tuple-element.18, f32[]{:T(128)} %get-tuple-element.19, f32[]{:T(128)} %get-tuple-element.20), channel_id=1, replica_groups=mesh['group_0'=8,'group_1'=2,'dev_0'=8,'dev_1'=8] {'dev_1'}, use_global_device_ids=true, to_apply=%region_4.0 | all-reduce | flops 4 | bytes 32 | tf_op jit(solution)/shard_map/psum | solution.py:41
  128.3 0.9 broadcast_multiply_fusion
  129.2 0.9 divide_add_fusion
  130.2 1.8 %copy.48 = f32[1,2,16,512]{3,2,1,0:T(8,128)} copy(f32[1,2,16,512]{2,3,1,0:T(8,128)} %get-tuple-element.30) | data formatting | bytes 131072
  132.0 0.8 copy.49
  132.8 0.0 copy-done.2
  132.8 0.1 add.97
  132.9 0.8 copy.47
  (28 shorter events, 0.4 us)
Async XLA Ops:
  0.6 4.7 %copy-start.5 = (f32[1,2,16,512]{3,2,1,0:T(8,128)S(1)}, f32[1,2,16,512]{3,2,1,0:T(8,128)}, u32[]{:S(2)}) copy-start(f32[1,2,16,512]{3,2,1,0:T(8,128)} %param.11) | copy-start | bytes 196612
  1.7 3.9 %copy-start.8 = (f32[512]{0:T(512)S(1)}, f32[512]{0:T(512)}, u32[]{:S(2)}) copy-start(f32[512]{0:T(512)} %constant.15.clone) | copy-start | bytes 6148
  5.7 6.2 %collective-permute-start = (f32[2,1,1,16,8,1,8]{3,6,5,4,2,1,0:T(8,128)S(1)}, f32[2,1,1,16,8,1,8]{3,6,5,4,2,1,0:T(8,128)S(1)}, u32[]{:S(2)}, u32[]{:S(2)}) collective-permute-start(f32[2,1,1,16,8,1,8]{3,6,5,4,2,1,0:T(8,128)S(1)} %pad_maximum_fusion.8), channel_id=1, source_target_pairs={{0,1},{1,2},{2,3},{3,4},{4,5},{5,6},{6,7},{7,8},{8,9},{9,10},{10,1... | collective-permute-start | bytes 24584 | tf_op jit(solution)/shard_map/ppermute | solution.py:33
  11.9 20.0 %collective-permute-start.1 = (f32[2,1,1,16,8,1,8]{3,6,5,4,2,1,0:T(8,128)S(1)}, f32[2,1,1,16,8,1,8]{3,6,5,4,2,1,0:T(8,128)S(1)}, u32[]{:S(2)}, u32[]{:S(2)}) collective-permute-start(f32[2,1,1,16,8,1,8]{3,6,5,4,2,1,0:T(8,128)S(1)} %get-tuple-element.35), channel_id=1, source_target_pairs={{1,0},{2,1},{3,2},{4,3},{5,4},{6,5},{7,6},{8,7},{9,8},{10,9},{11,1... | collective-permute-start | bytes 24584 | tf_op jit(solution)/shard_map/ppermute | solution.py:34
  32.1 4.4 %collective-permute-start.2 = (f32[2,1,2,16,1,8,8]{3,6,5,4,2,1,0:T(8,128)S(1)}, f32[2,1,2,16,1,8,8]{3,6,5,4,2,1,0:T(8,128)S(1)}, u32[]{:S(2)}, u32[]{:S(2)}) collective-permute-start(f32[2,1,2,16,1,8,8]{3,6,5,4,2,1,0:T(8,128)S(1)} %get-tuple-element.43), channel_id=1, source_target_pairs={{0,64},{64,128},{128,192},{192,256},{256,320},{320,384},{384,448},... | collective-permute-start | bytes 49160 | tf_op jit(solution)/shard_map/ppermute | solution.py:33
  32.1 4.4 %collective-permute-start.3 = (f32[2,1,2,16,1,8,8]{3,6,5,4,2,1,0:T(8,128)S(1)}, f32[2,1,2,16,1,8,8]{3,6,5,4,2,1,0:T(8,128)S(1)}, u32[]{:S(2)}, u32[]{:S(2)}) collective-permute-start(f32[2,1,2,16,1,8,8]{3,6,5,4,2,1,0:T(8,128)S(1)} %get-tuple-element.44), channel_id=1, source_target_pairs={{64,0},{128,64},{192,128},{256,192},{320,256},{384,320},{448,384},... | collective-permute-start | bytes 49160 | tf_op jit(solution)/shard_map/ppermute | solution.py:34
  38.1 4.8 %copy-start.4 = (bf16[1,2,16,512]{3,2,1,0:T(8,128)(2,1)S(1)}, bf16[1,2,16,512]{3,2,1,0:T(8,128)(2,1)}, u32[]{:S(2)}) copy-start(bf16[1,2,16,512]{3,2,1,0:T(8,128)(2,1)} %param.13) | copy-start | bytes 98308
  38.9 4.0 %copy-start = (f32[1536,512]{1,0:T(8,128)S(1)}, f32[1536,512]{1,0:T(8,128)}, u32[]{:S(2)}) copy-start(f32[1536,512]{1,0:T(8,128)} %constant.13.clone) | copy-start | bytes 9437188
  44.8 17.8 %copy-start.3 = (f32[1,2,16,512]{3,2,1,0:T(8,128)S(1)}, f32[1,2,16,512]{3,2,1,0:T(8,128)}, u32[]{:S(2)}) copy-start(f32[1,2,16,512]{3,2,1,0:T(8,128)} %param.10) | copy-start | bytes 196612
  44.8 19.0 %copy-start.6 = (f32[1,2,16,512]{3,2,1,0:T(8,128)S(1)}, f32[1,2,16,512]{3,2,1,0:T(8,128)}, u32[]{:S(2)}) copy-start(f32[1,2,16,512]{3,2,1,0:T(8,128)} %param.9) | copy-start | bytes 196612
  45.4 6.3 %collective-permute-start.5 = (f32[1,1,1,16,8,1,8]{3,6,5,4,2,1,0:T(8,128)S(1)}, f32[1,1,1,16,8,1,8]{3,6,5,4,2,1,0:T(8,128)S(1)}, u32[]{:S(2)}, u32[]{:S(2)}) collective-permute-start(f32[1,1,1,16,8,1,8]{3,6,5,4,2,1,0:T(8,128)S(1)} %bitcast.49), channel_id=1, source_target_pairs={{1,0},{2,1},{3,2},{4,3},{5,4},{6,5},{7,6},{8,7},{9,8},{10,9},{11,1... | collective-permute-start | bytes 12296 | tf_op jit(solution)/shard_map/ppermute | solution.py:34
  49.7 9.1 %collective-permute-start.4 = (f32[1,1,1,16,8,1,8]{3,6,5,4,2,1,0:T(8,128)S(1)}, f32[1,1,1,16,8,1,8]{3,6,5,4,2,1,0:T(8,128)S(1)}, u32[]{:S(2)}, u32[]{:S(2)}) collective-permute-start(f32[1,1,1,16,8,1,8]{3,6,5,4,2,1,0:T(8,128)S(1)} %bitcast.53), channel_id=1, source_target_pairs={{0,1},{1,2},{2,3},{3,4},{4,5},{5,6},{6,7},{7,8},{8,9},{9,10},{10,1... | collective-permute-start | bytes 12296 | tf_op jit(solution)/shard_map/ppermute | solution.py:33
  58.8 6.4 %copy-start.7 = (f32[8,8,8]{2,1,0:T(8,128)S(1)}, f32[8,8,8]{2,1,0:T(8,128)}, u32[]{:S(2)}) copy-start(f32[8,8,8]{2,1,0:T(8,128)} %constant.21) | copy-start | bytes 6148
  58.9 3.7 %collective-permute-start.6 = (f32[1,1,2,16,1,8,8]{3,6,5,4,2,1,0:T(8,128)S(1)}, f32[1,1,2,16,1,8,8]{3,6,5,4,2,1,0:T(8,128)S(1)}, u32[]{:S(2)}, u32[]{:S(2)}) collective-permute-start(f32[1,1,2,16,1,8,8]{3,6,5,4,2,1,0:T(8,128)S(1)} %pad_maximum_fusion.6), channel_id=1, source_target_pairs={{0,64},{64,128},{128,192},{192,256},{256,320},{320,384},{384,448},... | collective-permute-start | bytes 24584 | tf_op jit(solution)/shard_map/ppermute | solution.py:33
  62.6 1.9 %collective-permute-start.7 = (f32[1,1,2,16,1,8,8]{3,6,5,4,2,1,0:T(8,128)S(1)}, f32[1,1,2,16,1,8,8]{3,6,5,4,2,1,0:T(8,128)S(1)}, u32[]{:S(2)}, u32[]{:S(2)}) collective-permute-start(f32[1,1,2,16,1,8,8]{3,6,5,4,2,1,0:T(8,128)S(1)} %get-tuple-element.33), channel_id=1, source_target_pairs={{64,0},{128,64},{192,128},{256,192},{320,256},{384,320},{448,384},... | collective-permute-start | bytes 24584 | tf_op jit(solution)/shard_map/ppermute | solution.py:34
  64.1 2.3 %copy-start.1 = (f32[1,2,16,512]{2,3,1,0:T(8,128)S(1)}, f32[1,2,16,512]{2,3,1,0:T(8,128)}, u32[]{:S(2)}) copy-start(f32[1,2,16,512]{2,3,1,0:T(8,128)} %copy.36) | copy-start | bytes 196612
  129.2 3.6 %copy-start.2 = (f32[1,1,2,16,8,8,8]{3,6,5,4,2,1,0:T(8,128)S(1)}, f32[1,1,2,16,8,8,8]{3,6,5,4,2,1,0:T(8,128)}, u32[]{:S(2)}) copy-start(f32[1,1,2,16,8,8,8]{3,6,5,4,2,1,0:T(8,128)} %get-tuple-element.37) | copy-start | bytes 196612
where the time goes:
time: 134 us
  blocking collectives  57.2 us (43%)
  starting transfers between devices  30.2 us (23%)
  waiting for transfers between devices  17.8 us (13%)
  matrix products  8.93 us (7%)
  local copies, waits for them, and re-layouts  8.39 us (6%)
  other arithmetic  6.14 us (5%)
  between operations  5 us (4%)
    psum x4, blocking collectives, by_axis(): value = lax.psum(value, axis)  57.2 us
    ppermute x4, starting transfers between devices, extended(): after = lax.ppermute(initial, axis, down)  24.2 us
    ppermute x4, waiting for transfers between devices, extended(): before = lax.ppermute(last, axis, up)  15.5 us
    dot_general x3, matrix products, highest(): jnp.dot(left, right, precision=lax.Precision.HIGHEST, preferred_element_t...  8.93 us
    ppermute x4, starting transfers between devices, extended(): before = lax.ppermute(last, axis, up)  6.01 us
    unnamed x26, local copies, waits for them, and re-layouts  4.12 us
  transfers between devices with their start and end apart: 8, of which 6 were waited for; matrix products, arithmetic and copies ran while one was open for 1% of the time, Pallas kernels for 0%

commit v1 on v0

v1 whole, which is shorter than its diff:
```python
import jax
import jax.numpy as jnp
import numpy as np
from jax import lax
from jax.experimental import pallas as pl
from jax.experimental.pallas import tpu as pltpu
from jax.sharding import PartitionSpec as P

NP = 8
LANES = 128
TILES = NP**3 // LANES
HALF = NP * NP

lobatto_nodes = [
    -1.0,
    -0.8717401485096066,
    -0.5917001814331423,
    -0.2092992179024789,
    0.2092992179024789,
    0.5917001814331423,
    0.8717401485096066,
    1.0,
]


def derivative_table():
    nodes = np.array(lobatto_nodes)
    identity = np.eye(NP)
    offset = nodes[:, None] - nodes[None, :] + identity
    barycentric = 1.0 / np.prod(offset, axis=1)
    derivative = barycentric[None, :] / barycentric[:, None] / offset * (1.0 - identity)
    return derivative - identity * np.sum(derivative, axis=1)[:, None]


def lane_tables():
    derivative = derivative_table()
    half = np.arange(LANES) // HALF
    rows = []
    for matrix in (derivative, derivative.T):
        for out in range(TILES):
            for inp in range(TILES):
                rows.append(matrix[2 * out + half, 2 * inp + half])
                rows.append(matrix[2 * out + half, 2 * inp + 1 - half])
    edge = np.where(np.arange(NP) % (NP - 1) == 0, 0.5, 1.0)
    rows.extend(np.kron(np.kron(edge, edge), edge).reshape(TILES, LANES))
    rows.extend(np.zeros((72 - len(rows), LANES)))
    return np.stack(rows).astype(np.float32)


def plane_table():
    derivative = derivative_table()
    identity = np.eye(NP)
    along_j = np.kron(np.eye(2), np.kron(derivative, identity))
    along_k = np.kron(np.eye(2), np.kron(identity, derivative))
    return np.concatenate([along_j.T, along_k.T], axis=1).astype(np.float32)


def lanes(rows):
    return lax.broadcasted_iota(jnp.int32, (rows, LANES), 1)


def roll(value, shift, axis):
    return pltpu.roll(value, shift % value.shape[axis], axis)


def split(value, dims):
    eb, ez = dims
    return [
        [value[b * ez : (b + 1) * ez, t * LANES : (t + 1) * LANES] for b in range(eb)]
        for t in range(TILES)
    ]


def join(blocks):
    return jnp.concatenate([jnp.concatenate(tile, axis=0) for tile in blocks], axis=1)


def local_assemble(blocks):
    result = []
    for tile in blocks:
        lane = lanes(tile[0].shape[0])
        k = lane % NP
        j = (lane // NP) % NP
        summed = []
        for x in tile:
            above = roll(roll(x, NP - 1, 1), -1, 0)
            below = roll(roll(x, 1 - NP, 1), 1, 0)
            summed.append(x + jnp.where(k == NP - 1, above, jnp.where(k == 0, below, 0.0)))
        out = []
        last = len(summed) - 1
        for b, x in enumerate(summed):
            y = x
            if b < last:
                y = y + jnp.where(j == NP - 1, roll(summed[b + 1], HALF - NP, 1), 0.0)
            if b > 0:
                y = y + jnp.where(j == 0, roll(summed[b - 1], NP - HALF, 1), 0.0)
            out.append(y)
        result.append(out)
    return result


def pack_dev(fields, block, node):
    rows = fields[0][0][block].shape[0]
    lane = lanes(rows)
    packed = jnp.zeros((rows, LANES), jnp.float32)
    for f, blocks in enumerate(fields):
        for i in range(NP):
            t, h = divmod(i, 2)
            target = f * HALF + i * NP
            source = h * HALF + node * NP
            moved = roll(blocks[t][block], target - source, 1)
            packed = jnp.where(lane // NP == target // NP, moved, packed)
    return packed


def unpack_dev(packed, field, node, tile):
    lane = lanes(packed.shape[0])
    result = jnp.zeros(packed.shape, jnp.float32)
    for h in range(2):
        source = field * HALF + (2 * tile + h) * NP
        target = h * HALF + node * NP
        result = jnp.where(lane // NP == target // NP, roll(packed, target - source, 1), result)
    return result


def pack_group(fields, upper):
    tile = TILES - 1 if upper else 0
    parts = [jnp.concatenate(blocks[tile], axis=0) for blocks in fields]
    lane = lanes(parts[0].shape[0])
    if upper:
        parts[0] = roll(parts[0], HALF, 1)
    else:
        parts[1:] = [roll(part, HALF, 1) for part in parts[1:]]
    other = parts[1] if len(parts) > 1 else 0.0
    return jnp.where(lane < HALF, parts[0], other)


def add_dev(blocks, field, before, after):
    out = []
    for t, tile in enumerate(blocks):
        tile = list(tile)
        tile[0] = tile[0] + unpack_dev(before, field, 0, t)
        tile[-1] = tile[-1] + unpack_dev(after, field, NP - 1, t)
        out.append(tile)
    return out


def add_group(blocks, field, before, after):
    eb = len(blocks[0])
    ez = blocks[0][0].shape[0]
    lane = lanes(ez)
    out = [list(tile) for tile in blocks]
    for b in range(eb):
        low = before[b * ez : (b + 1) * ez, :]
        high = after[b * ez : (b + 1) * ez, :]
        if field:
            low = roll(low, HALF, 1)
        else:
            high = roll(high, HALF, 1)
        out[0][b] = out[0][b] + jnp.where(lane < HALF, low, 0.0)
        out[-1][b] = out[-1][b] + jnp.where(lane >= HALF, high, 0.0)
    return out


def first_direction(tables, base, tiles, squared=False):
    swapped = [roll(tile, HALF, 1) for tile in tiles]
    out = []
    for o in range(TILES):
        acc = None
        for i in range(TILES):
            row = base + 2 * (o * TILES + i)
            same = tables[row : row + 1, :]
            other = tables[row + 1 : row + 2, :]
            if squared:
                same, other = same * same, other * other
            term = same * tiles[i] + other * swapped[i]
            acc = term if acc is None else acc + term
        out.append(acc)
    return out


def matmul(left, right):
    return lax.dot_general(
        left,
        right,
        (((1,), (0,)), ((), ())),
        precision=lax.Precision.HIGHEST,
        preferred_element_type=jnp.float32,
    )


def matmul_t(left, right):
    return lax.dot_general(
        left,
        right,
        (((1,), (1,)), ((), ())),
        precision=lax.Precision.HIGHEST,
        preferred_element_type=jnp.float32,
    )


def tiles_of(value):
    return [value[:, t * LANES : (t + 1) * LANES] for t in range(TILES)]


def stack_rows(tiles):
    return jnp.concatenate(tiles, axis=0)


def unstack_rows(value):
    rows = value.shape[0] // TILES
    return [value[t * rows : (t + 1) * rows, :] for t in range(TILES)]


def blocks_of(tiles, dims):
    eb, ez = dims
    return [[tile[b * ez : (b + 1) * ez, :] for b in range(eb)] for tile in tiles]


def start_kernel(dims, direction, tables, field_out, dev_low, dev_high, group_low, group_high):
    weighted = [
        tables[64 + t : 65 + t, :] * direction[:, t * LANES : (t + 1) * LANES] for t in range(TILES)
    ]
    blocks = local_assemble(blocks_of(weighted, dims))
    field_out[...] = join(blocks)
    dev_low[...] = pack_dev([blocks], 0, 0)
    dev_high[...] = pack_dev([blocks], dims[0] - 1, NP - 1)
    group_low[...] = pack_group([blocks], False)
    group_high[...] = pack_group([blocks], True)


def diagonal_kernel(dims, geometry, mass, plane, tables, diag_out):
    geo = [tiles_of(geometry[c].astype(jnp.float32)) for c in range(3)]
    first = first_direction(tables, 32, geo[0], squared=True)
    table = plane[...]
    pair = jnp.concatenate([stack_rows(geo[1]), stack_rows(geo[2])], axis=1)
    rest = unstack_rows(matmul_t(pair, table * table))
    masses = tiles_of(mass[...].astype(jnp.float32))
    local = [a + b + c for a, b, c in zip(first, rest, masses)]
    diag_out[...] = join(local_assemble(blocks_of(local, dims)))


def corner_kernel(dims, group_low, group_high, before, after, low_out, high_out):
    eb, ez = dims
    low_recv = before[...]
    high_recv = after[...]
    lane = lanes(ez)
    j = (lane // NP) % NP
    for ref, out, upper in ((group_low, low_out, False), (group_high, high_out, True)):
        shift_low = NP - HALF if upper else 0
        shift_high = 0 if upper else HALF - NP
        blocks = [ref[b * ez : (b + 1) * ez, :] for b in range(eb)]
        low = roll(low_recv, shift_low, 1) if shift_low else low_recv
        high = roll(high_recv, shift_high, 1) if shift_high else high_recv
        blocks[0] = blocks[0] + jnp.where(j == 0, low, 0.0)
        blocks[-1] = blocks[-1] + jnp.where(j == NP - 1, high, 0.0)
        for b in range(eb):
            out[b * ez : (b + 1) * ez, :] = blocks[b]


def operator_kernel(
    dims,
    field,
    dev_before,
    dev_after,
    group_before,
    group_after,
    geometry,
    mass,
    plane,
    tables,
    diag,
    smooth_out,
    applied_out,
    dev_low,
    dev_high,
    group_low,
    group_high,
):
    blocks = split(field, dims)
    blocks = add_dev(blocks, 0, dev_before[...], dev_after[...])
    blocks = add_group(blocks, 0, group_before, group_after)
    smooth_out[...] = join(blocks)
    tiles = [jnp.concatenate(tile, axis=0) for tile in blocks]
    geo = [tiles_of(geometry[c].astype(jnp.float32)) for c in range(3)]
    table = plane[...]
    first = [g * f for g, f in zip(geo[0], first_direction(tables, 0, tiles))]
    gradient = matmul(stack_rows(tiles), table)
    pair = jnp.concatenate([stack_rows(geo[1]), stack_rows(geo[2])], axis=1) * gradient
    rest = unstack_rows(matmul_t(pair, table))
    first = first_direction(tables, 32, first)
    masses = tiles_of(mass[...].astype(jnp.float32))
    local = [a + b + m * u for a, b, m, u in zip(first, rest, masses, tiles)]
    blocks = local_assemble(blocks_of(local, dims))
    applied_out[...] = join(blocks)
    diag_blocks = split(diag, dims)
    dev_low[...] = pack_dev([blocks, diag_blocks], 0, 0)
    dev_high[...] = pack_dev([blocks, diag_blocks], dims[0] - 1, NP - 1)
    group_low[...] = pack_group([blocks, diag_blocks], False)
    group_high[...] = pack_group([blocks, diag_blocks], True)


def products_kernel(
    dims,
    field,
    diag,
    dev_before,
    dev_after,
    group_before,
    group_after,
    residual,
    smooth,
    tables,
    applied_out,
    inverse_out,
    sums_out,
):
    full = []
    for index, ref in enumerate((field, diag)):
        blocks = add_dev(split(ref, dims), index, dev_before[...], dev_after[...])
        blocks = add_group(blocks, index, group_before, group_after)
        full.append([jnp.concatenate(tile, axis=0) for tile in blocks])
    sums = [None] * 4
    for t in range(TILES):
        window = slice(t * LANES, (t + 1) * LANES)
        weight = tables[64 + t : 65 + t, :]
        applied = full[0][t]
        inverse = 1.0 / full[1][t]
        applied_out[:, window] = applied
        inverse_out[:, window] = inverse
        res = residual[:, window]
        weighted = weight * inverse
        terms = (
            weighted * res * res,
            weight * smooth[:, window] * applied,
            weighted * res * applied,
            weighted * applied * applied,
        )
        sums = [term if s is None else s + term for s, term in zip(sums, terms)]
    lane = lanes(1)
    row = jnp.zeros((1, LANES), jnp.float32)
    for n, total in enumerate(sums):
        column = jnp.sum(total, axis=0, keepdims=True)
        row = jnp.where(lane == n, jnp.sum(column, axis=1, keepdims=True), row)
    sums_out[...] = jnp.broadcast_to(row.reshape(1, 1, LANES), sums_out.shape)


def middle_kernel(parts, sums_out):
    total = jnp.sum(parts[...], axis=0, keepdims=True)
    sums_out[...] = jnp.broadcast_to(total, sums_out.shape)


def final_kernel(
    parts, solution, residual, smooth, applied, inverse, solution_out, residual_out, direction_out
):
    total = jnp.sum(parts[...], axis=0)
    norm_now, curvature, cross, quad = (total[:, n : n + 1] for n in range(4))
    step = norm_now / curvature
    norm_next = norm_now - 2.0 * step * cross + step * step * quad
    ratio = norm_next / norm_now
    direction = smooth[...]
    res = residual[...] - step * applied[...]
    solution_out[...] = solution[...] + step * direction
    residual_out[...] = res
    direction_out[...] = res * inverse[...] + ratio * direction


def call(kernel, shapes, *args):
    outs = tuple(jax.ShapeDtypeStruct(shape, jnp.float32) for shape in shapes)
    vmem = pl.BlockSpec(memory_space=pltpu.VMEM)
    return pl.pallas_call(
        kernel,
        out_shape=outs,
        in_specs=[vmem] * len(args),
        out_specs=(vmem,) * len(outs),
        compiler_params=pltpu.CompilerParams(vmem_limit_bytes=8 * 2**20),
    )(*args)


def both_ways(low, high, axis):
    peers = lax.axis_size(axis)
    up = [(i, (i + 1) % peers) for i in range(peers)]
    before = lax.ppermute(high, axis, up)
    after = lax.ppermute(low, axis, [(j, i) for i, j in up])
    return before, after


def solution(mesh):
    groups = mesh.shape["group"]
    devs = mesh.shape["dev"]

    def on_device(solution, residual, direction, geometry, mass):
        local = solution.shape
        dims = local[1:3]
        rows = dims[0] * dims[1]
        points = local[3]
        flat = (rows, points)
        face_dev = (dims[1], LANES)
        face_group = (rows, LANES)
        solution, residual, direction, mass = (
            array.reshape(flat) for array in (solution, residual, direction, mass)
        )
        geometry = geometry.reshape((3,) + flat)
        tables = jnp.asarray(lane_tables())
        plane = jnp.asarray(plane_table())

        def bind(kernel):
            def body(*refs):
                kernel(dims, *refs)

            body.__name__ = kernel.__name__
            return body

        corners = bind(corner_kernel)
        field, dev_low, dev_high, group_low, group_high = call(
            bind(start_kernel),
            [flat, face_dev, face_dev, face_group, face_group],
            direction,
            tables,
        )
        dev = both_ways(dev_low, dev_high, "dev")
        (diag,) = call(bind(diagonal_kernel), [flat], geometry, mass, plane, tables)
        low, high = call(corners, [face_group] * 2, group_low, group_high, *dev)
        group = both_ways(low, high, "group")
        smooth, applied, dev_low, dev_high, group_low, group_high = call(
            bind(operator_kernel),
            [flat, flat, face_dev, face_dev, face_group, face_group],
            field,
            *dev,
            *group,
            geometry,
            mass,
            plane,
            tables,
            diag,
        )
        dev = both_ways(dev_low, dev_high, "dev")
        low, high = call(corners, [face_group] * 2, group_low, group_high, *dev)
        group = both_ways(low, high, "group")
        applied, inverse, sums = call(
            bind(products_kernel),
            [flat, flat, (devs, 1, LANES)],
            applied,
            diag,
            *dev,
            *group,
            residual,
            smooth,
            tables,
        )
        sums = lax.all_to_all(sums, "dev", 0, 0)
        (sums,) = call(middle_kernel, [(groups, 1, LANES)], sums)
        sums = lax.all_to_all(sums, "group", 0, 0)
        outs = call(
            final_kernel, [flat] * 3, sums, solution, residual, smooth, applied, inverse
        )
        return tuple(out.reshape(local) for out in outs)

    spec = P("group", "dev", None, None)
    return jax.shard_map(
        on_device,
        mesh=mesh,
        in_specs=(spec, spec, spec, P(None, "group", "dev", None, None), spec),
        out_specs=(spec, spec, spec),
        check_vma=False,
    )
```

time: 134 us -> 84.8 us (0.63)
  the two profiles are of different devices: /device:TPU:18 before, /device:TPU:1 now
where the time goes in v1:
time: 84.8 us; the launch traced here: 84.2 us
  starting transfers between devices  36.4 us (43%)
  blocking collectives  35.4 us (42%)
  waiting for transfers between devices  5.58 us (7%)
  local copies, waits for them, and re-layouts  3.29 us (4%)
  Pallas kernels  2.84 us (3%)
    ppermute x4, starting transfers between devices, both_ways(): after = lax.ppermute(low, axis, [(j, i) for i, j in up])  25.5 us
    all_to_all x1, blocking collectives, on_device(): sums = lax.all_to_all(sums, 'dev', 0, 0)  18.4 us
    all_to_all x1, blocking collectives, on_device(): sums = lax.all_to_all(sums, 'group', 0, 0)  17 us
    ppermute x4, starting transfers between devices, both_ways(): before = lax.ppermute(high, axis, up)  10.8 us
    ppermute x4, waiting for transfers between devices, both_ways(): after = lax.ppermute(low, axis, [(j, i) for i, j in up])  4.86 us
    unnamed x18, local copies, waits for them, and re-layouts  3.29 us
    pallas_call x8, Pallas kernels, call(): pl.pallas_call(kernel, out_shape=outs, in_specs=[vmem] * len(args), out_s...  2.84 us
  transfers between devices with their start and end apart: 8, of which 5 were waited for; matrix products, arithmetic and copies ran while one was open for 0% of the time, Pallas kernels for 1%

profile of v1, /device:TPU:1, one launch (start us, length us, event | category | flops | bytes accessed | tf_op | source)
XLA Modules:
  0.0 84.2 jit_solution(1570936054600734026)
XLA Ops:
  0.6 0.0 copy-start
  0.6 0.8 copy-done
  1.4 0.0 copy-start.7
  1.4 0.8 copy-done.7
  2.2 0.0 copy-start.4
  2.2 0.2 shard_map.94
  2.5 0.0 copy-start.1
  2.5 3.9 %collective-permute-start = (f32[16,128]{1,0:T(8,128)S(1)}, f32[16,128]{1,0:T(8,128)S(1)}, u32[]{:S(2)}, u32[]{:S(2)}) collective-permute-start(f32[16,128]{1,0:T(8,128)S(1)} %get-tuple-element.25), channel_id=1, source_target_pairs={{0,1},{1,2},{2,3},{3,4},{4,5},{5,6},{6,7},{7,8},{8,9},{9,10},{10,1... | collective-permute-start | bytes 24584 | tf_op jit(solution)/shard_map/ppermute | solution.py:383
  6.5 18.1 %collective-permute-start.1 = (f32[16,128]{1,0:T(8,128)S(1)}, f32[16,128]{1,0:T(8,128)S(1)}, u32[]{:S(2)}, u32[]{:S(2)}) collective-permute-start(f32[16,128]{1,0:T(8,128)S(1)} %get-tuple-element.26), channel_id=1, source_target_pairs={{1,0},{2,1},{3,2},{4,3},{5,4},{6,5},{7,6},{8,7},{9,8},{10,9},{11,1... | collective-permute-start | bytes 24584 | tf_op jit(solution)/shard_map/ppermute | solution.py:384
  24.6 0.0 collective-permute-done.refs_2_.refs_1_
  24.6 0.8 collective-permute-done.1.refs_3_.refs_2_
  25.4 0.1 shard_map.95
  25.4 2.8 %collective-permute-start.2 = (f32[32,128]{1,0:T(8,128)S(1)}, f32[32,128]{1,0:T(8,128)S(1)}, u32[]{:S(2)}, u32[]{:S(2)}) collective-permute-start(f32[32,128]{1,0:T(8,128)S(1)} %get-tuple-element.29), channel_id=1, source_target_pairs={{0,64},{64,128},{128,192},{192,256},{256,320},{320,384},{384,448},... | collective-permute-start | bytes 49160 | tf_op jit(solution)/shard_map/ppermute | solution.py:383
  28.3 0.0 collective-permute-start.3
  28.3 0.0 copy-done.4
  28.3 0.0 copy-done.1
  28.3 0.0 copy-start.2
  28.3 0.9 %copy-done.2 = f32[128,256]{1,0:T(8,128)S(1)} copy-done((f32[128,256]{1,0:T(8,128)S(1)}, f32[128,256]{1,0:T(8,128)}, u32[]{:S(2)}) %copy-start.2) | copy-done | bytes 131096
  29.2 0.0 copy-start.6
  29.2 0.8 copy-done.6
  30.0 0.0 copy-start.3
  30.0 0.4 shard_map.96.refs_9_.refs_1_
  30.4 0.0 collective-permute-done.2.refs_3_
  30.4 1.0 %collective-permute-done.3.refs_4_ = f32[32,128]{1,0:T(8,128)S(1)} collective-permute-done((f32[32,128]{1,0:T(8,128)S(1)}, f32[32,128]{1,0:T(8,128)S(1)}, u32[]{:S(2)}, u32[]{:S(2)}) %collective-permute-start.3) | collective-permute-done | bytes 16416 | tf_op jit(solution)/shard_map/ppermute | solution.py:384
  31.4 0.0 copy-done.3
  31.4 0.9 %shard_map.97 = (f32[32,512]{1,0:T(8,128)S(1)}, f32[32,512]{1,0:T(8,128)S(1)}, f32[16,128]{1,0:T(8,128)S(1)}, f32[16,128]{1,0:T(8,128)S(1)}, f32[32,128]{1,0:T(8,128)S(1)}, /*index=5*/f32[32,128]{1,0:T(8,128)S(1)}) custom-call(f32[32,512]{1,0:T(8,128)S(1)} %get-tuple-element.24.refs_0_, f32[16,128]{1,0:T(8,128)S(1)} %collective-permute-done.refs_2_.refs_1_, ...), custom_call_target="tpu_custom_call" | custom-call | tf_op jit(solution)/shard_map/pallas_call | solution.py:371
  32.4 0.0 copy-start.5
  32.4 2.1 %collective-permute-start.4 = (f32[16,128]{1,0:T(8,128)S(1)}, f32[16,128]{1,0:T(8,128)S(1)}, u32[]{:S(2)}, u32[]{:S(2)}) collective-permute-start(f32[16,128]{1,0:T(8,128)S(1)} %get-tuple-element.32), channel_id=1, source_target_pairs={{0,1},{1,2},{2,3},{3,4},{4,5},{5,6},{6,7},{7,8},{8,9},{9,10},{10,1... | collective-permute-start | bytes 24584 | tf_op jit(solution)/shard_map/ppermute | solution.py:383
  34.4 7.2 %collective-permute-start.5 = (f32[16,128]{1,0:T(8,128)S(1)}, f32[16,128]{1,0:T(8,128)S(1)}, u32[]{:S(2)}, u32[]{:S(2)}) collective-permute-start(f32[16,128]{1,0:T(8,128)S(1)} %get-tuple-element.33), channel_id=1, source_target_pairs={{1,0},{2,1},{3,2},{4,3},{5,4},{6,5},{7,6},{8,7},{9,8},{10,9},{11,1... | collective-permute-start | bytes 24584 | tf_op jit(solution)/shard_map/ppermute | solution.py:384
  41.7 0.0 collective-permute-done.4.refs_2_
  41.7 0.8 collective-permute-done.5.refs_3_
  42.4 0.1 shard_map.98
  42.5 2.0 %collective-permute-start.6 = (f32[32,128]{1,0:T(8,128)S(1)}, f32[32,128]{1,0:T(8,128)S(1)}, u32[]{:S(2)}, u32[]{:S(2)}) collective-permute-start(f32[32,128]{1,0:T(8,128)S(1)} %get-tuple-element.36), channel_id=1, source_target_pairs={{0,64},{64,128},{128,192},{192,256},{256,320},{320,384},{384,448},... | collective-permute-start | bytes 49160 | tf_op jit(solution)/shard_map/ppermute | solution.py:383
  44.5 0.2 collective-permute-start.7
  44.7 0.7 collective-permute-done.6.refs_4_
  45.4 2.3 %collective-permute-done.7.refs_5_ = f32[32,128]{1,0:T(8,128)S(1)} collective-permute-done((f32[32,128]{1,0:T(8,128)S(1)}, f32[32,128]{1,0:T(8,128)S(1)}, u32[]{:S(2)}, u32[]{:S(2)}) %collective-permute-start.7) | collective-permute-done | bytes 16416 | tf_op jit(solution)/shard_map/ppermute | solution.py:384
  47.7 0.0 copy-done.5
  47.7 0.2 shard_map.99
  47.9 0.0 copy-start.8
  47.9 18.4 %all_to_all.10.parts = f32[64,1,128]{2,1,0:T(1,128)S(1)} all-to-all(f32[64,1,128]{2,1,0:T(1,128)S(1)} %get-tuple-element.39), channel_id=1, replica_groups=mesh['group'=16,'dev'=64] {'dev'}, dimensions={0} | all-to-all | bytes 65536 | tf_op jit(solution)/shard_map/all_to_all | solution.py:451
  66.4 0.1 shard_map.100
  66.4 17.0 %all_to_all.11.parts = f32[16,1,128]{2,1,0:T(1,128)S(1)} all-to-all(f32[16,1,128]{2,1,0:T(1,128)S(1)} %shard_map.100), channel_id=1, replica_groups=mesh['group'=16,'dev'=64] {'group'}, dimensions={0} | all-to-all | bytes 16384 | tf_op jit(solution)/shard_map/all_to_all | solution.py:453
  83.4 0.0 copy-done.8
  83.4 0.8 shard_map.101
Async XLA Ops:
  0.6 0.8 copy-start
  1.4 0.8 copy-start.7
  2.2 26.0 %copy-start.4 = (bf16[3,1,2,16,512]{4,3,2,1,0:T(8,128)(2,1)S(1)}, bf16[3,1,2,16,512]{4,3,2,1,0:T(8,128)(2,1)}, u32[]{:S(2)}) copy-start(bf16[3,1,2,16,512]{4,3,2,1,0:T(8,128)(2,1)} %param.10) | copy-start | bytes 294916
  2.5 25.8 %copy-start.1 = (f32[72,128]{1,0:T(8,128)S(1)}, f32[72,128]{1,0:T(8,128)}, u32[]{:S(2)}) copy-start(f32[72,128]{1,0:T(8,128)} %constant.4.clone.refs_1_.refs_3_.refs_8_) | copy-start | bytes 110596
  2.5 22.1 %collective-permute-start = (f32[16,128]{1,0:T(8,128)S(1)}, f32[16,128]{1,0:T(8,128)S(1)}, u32[]{:S(2)}, u32[]{:S(2)}) collective-permute-start(f32[16,128]{1,0:T(8,128)S(1)} %get-tuple-element.25), channel_id=1, source_target_pairs={{0,1},{1,2},{2,3},{3,4},{4,5},{5,6},{6,7},{7,8},{8,9},{9,10},{10,1... | collective-permute-start | bytes 24584 | tf_op jit(solution)/shard_map/ppermute | solution.py:383
  6.5 18.9 %collective-permute-start.1 = (f32[16,128]{1,0:T(8,128)S(1)}, f32[16,128]{1,0:T(8,128)S(1)}, u32[]{:S(2)}, u32[]{:S(2)}) collective-permute-start(f32[16,128]{1,0:T(8,128)S(1)} %get-tuple-element.26), channel_id=1, source_target_pairs={{1,0},{2,1},{3,2},{4,3},{5,4},{6,5},{7,6},{8,7},{9,8},{10,9},{11,1... | collective-permute-start | bytes 24584 | tf_op jit(solution)/shard_map/ppermute | solution.py:384
  25.4 4.9 %collective-permute-start.2 = (f32[32,128]{1,0:T(8,128)S(1)}, f32[32,128]{1,0:T(8,128)S(1)}, u32[]{:S(2)}, u32[]{:S(2)}) collective-permute-start(f32[32,128]{1,0:T(8,128)S(1)} %get-tuple-element.29), channel_id=1, source_target_pairs={{0,64},{64,128},{128,192},{192,256},{256,320},{320,384},{384,448},... | collective-permute-start | bytes 49160 | tf_op jit(solution)/shard_map/ppermute | solution.py:383
  28.3 3.2 %collective-permute-start.3 = (f32[32,128]{1,0:T(8,128)S(1)}, f32[32,128]{1,0:T(8,128)S(1)}, u32[]{:S(2)}, u32[]{:S(2)}) collective-permute-start(f32[32,128]{1,0:T(8,128)S(1)} %get-tuple-element.30), channel_id=1, source_target_pairs={{64,0},{128,64},{192,128},{256,192},{320,256},{384,320},{448,384},... | collective-permute-start | bytes 49160 | tf_op jit(solution)/shard_map/ppermute | solution.py:384
  28.3 0.9 %copy-start.2 = (f32[128,256]{1,0:T(8,128)S(1)}, f32[128,256]{1,0:T(8,128)}, u32[]{:S(2)}) copy-start(f32[128,256]{1,0:T(8,128)} %constant.5.clone.refs_2_.refs_7_) | copy-start | bytes 393220
  29.2 0.8 copy-start.6
  30.0 1.5 %copy-start.3 = (f32[128,256]{1,0:T(8,128)S(1)}, f32[128,256]{1,0:T(8,128)}, u32[]{:S(2)}) copy-start(f32[128,256]{1,0:T(8,128)} %constant.5.clone.refs_2_.refs_7_) | copy-start | bytes 393220
  32.4 15.3 %copy-start.5 = (f32[1,2,16,512]{3,2,1,0:T(8,128)S(1)}, f32[1,2,16,512]{3,2,1,0:T(8,128)}, u32[]{:S(2)}) copy-start(f32[1,2,16,512]{3,2,1,0:T(8,128)} %param.8) | copy-start | bytes 196612
  32.4 9.3 %collective-permute-start.4 = (f32[16,128]{1,0:T(8,128)S(1)}, f32[16,128]{1,0:T(8,128)S(1)}, u32[]{:S(2)}, u32[]{:S(2)}) collective-permute-start(f32[16,128]{1,0:T(8,128)S(1)} %get-tuple-element.32), channel_id=1, source_target_pairs={{0,1},{1,2},{2,3},{3,4},{4,5},{5,6},{6,7},{7,8},{8,9},{9,10},{10,1... | collective-permute-start | bytes 24584 | tf_op jit(solution)/shard_map/ppermute | solution.py:383
  34.4 8.0 %collective-permute-start.5 = (f32[16,128]{1,0:T(8,128)S(1)}, f32[16,128]{1,0:T(8,128)S(1)}, u32[]{:S(2)}, u32[]{:S(2)}) collective-permute-start(f32[16,128]{1,0:T(8,128)S(1)} %get-tuple-element.33), channel_id=1, source_target_pairs={{1,0},{2,1},{3,2},{4,3},{5,4},{6,5},{7,6},{8,7},{9,8},{10,9},{11,1... | collective-permute-start | bytes 24584 | tf_op jit(solution)/shard_map/ppermute | solution.py:384
  42.5 2.9 %collective-permute-start.6 = (f32[32,128]{1,0:T(8,128)S(1)}, f32[32,128]{1,0:T(8,128)S(1)}, u32[]{:S(2)}, u32[]{:S(2)}) collective-permute-start(f32[32,128]{1,0:T(8,128)S(1)} %get-tuple-element.36), channel_id=1, source_target_pairs={{0,64},{64,128},{128,192},{192,256},{256,320},{320,384},{384,448},... | collective-permute-start | bytes 49160 | tf_op jit(solution)/shard_map/ppermute | solution.py:383
  44.5 3.2 %collective-permute-start.7 = (f32[32,128]{1,0:T(8,128)S(1)}, f32[32,128]{1,0:T(8,128)S(1)}, u32[]{:S(2)}, u32[]{:S(2)}) collective-permute-start(f32[32,128]{1,0:T(8,128)S(1)} %get-tuple-element.37), channel_id=1, source_target_pairs={{64,0},{128,64},{192,128},{256,192},{320,256},{384,320},{448,384},... | collective-permute-start | bytes 49160 | tf_op jit(solution)/shard_map/ppermute | solution.py:384
  47.9 35.5 %copy-start.8 = (f32[1,2,16,512]{3,2,1,0:T(8,128)S(1)}, f32[1,2,16,512]{3,2,1,0:T(8,128)}, u32[]{:S(2)}) copy-start(f32[1,2,16,512]{3,2,1,0:T(8,128)} %param.7) | copy-start | bytes 196612

commit v2 on v1

--- a/solution.py
+++ b/solution.py
@@ -10,6 +10,7 @@
 LANES = 128
 TILES = NP**3 // LANES
 HALF = NP * NP
+SECOND = 64
 
 lobatto_nodes = [
     -1.0,
@@ -41,22 +42,39 @@
             for inp in range(TILES):
                 rows.append(matrix[2 * out + half, 2 * inp + half])
                 rows.append(matrix[2 * out + half, 2 * inp + 1 - half])
-    edge = np.where(np.arange(NP) % (NP - 1) == 0, 0.5, 1.0)
-    rows.extend(np.kron(np.kron(edge, edge), edge).reshape(TILES, LANES))
-    rows.extend(np.zeros((72 - len(rows), LANES)))
+    lane = np.arange(LANES)
+    rows.extend(derivative[(lane // NP) % NP, node] for node in range(NP))
+    rows.extend(derivative[lane % NP, node] for node in range(NP))
     return np.stack(rows).astype(np.float32)
-
-
-def plane_table():
-    derivative = derivative_table()
-    identity = np.eye(NP)
-    along_j = np.kron(np.eye(2), np.kron(derivative, identity))
-    along_k = np.kron(np.eye(2), np.kron(identity, derivative))
-    return np.concatenate([along_j.T, along_k.T], axis=1).astype(np.float32)
 
 
 def lanes(rows):
     return lax.broadcasted_iota(jnp.int32, (rows, LANES), 1)
+
+
+def plane_table(tables):
+    lane = lanes(NP)
+    sub = lax.broadcasted_iota(jnp.int32, (NP, LANES), 0)
+    same_k = lane % NP == sub
+    along_k = tables[SECOND + NP : SECOND + 2 * NP, :]
+    parts_j, parts_k = [], []
+    for block in range(LANES // NP):
+        half, j = divmod(block, NP)
+        along_j = jnp.broadcast_to(tables[SECOND + j : SECOND + j + 1, :], (NP, LANES))
+        parts_j.append(jnp.where(same_k & (lane // HALF == half), along_j, 0.0))
+        parts_k.append(jnp.where(lane // NP == block, along_k, 0.0))
+    return jnp.concatenate(
+        [jnp.concatenate(parts_j, axis=0), jnp.concatenate(parts_k, axis=0)], axis=1
+    )
+
+
+def lane_weights(tile):
+    lane = lanes(1)
+    i = 2 * tile + lane // HALF
+    weight = jnp.ones((1, LANES), jnp.float32)
+    for node in (i, (lane // NP) % NP, lane % NP):
+        weight = weight * jnp.where((node == 0) | (node == NP - 1), 0.5, 1.0)
+    return weight
 
 
 def roll(value, shift, axis):
@@ -217,9 +235,9 @@
     return [[tile[b * ez : (b + 1) * ez, :] for b in range(eb)] for tile in tiles]
 
 
-def start_kernel(dims, direction, tables, field_out, dev_low, dev_high, group_low, group_high):
+def start_kernel(dims, direction, field_out, dev_low, dev_high, group_low, group_high):
     weighted = [
-        tables[64 + t : 65 + t, :] * direction[:, t * LANES : (t + 1) * LANES] for t in range(TILES)
+        lane_weights(t) * direction[:, t * LANES : (t + 1) * LANES] for t in range(TILES)
     ]
     blocks = local_assemble(blocks_of(weighted, dims))
     field_out[...] = join(blocks)
@@ -229,10 +247,12 @@
     group_high[...] = pack_group([blocks], True)
 
 
-def diagonal_kernel(dims, geometry, mass, plane, tables, diag_out):
+def diagonal_kernel(dims, geometry, mass, tables, diag_out, tables_out, plane_out):
     geo = [tiles_of(geometry[c].astype(jnp.float32)) for c in range(3)]
     first = first_direction(tables, 32, geo[0], squared=True)
-    table = plane[...]
+    table = plane_table(tables)
+    tables_out[...] = tables[...]
+    plane_out[...] = table
     pair = jnp.concatenate([stack_rows(geo[1]), stack_rows(geo[2])], axis=1)
     rest = unstack_rows(matmul_t(pair, table * table))
     masses = tiles_of(mass[...].astype(jnp.float32))
@@ -267,8 +287,8 @@
     group_after,
     geometry,
     mass,
+    tables,
     plane,
-    tables,
     diag,
     smooth_out,
     applied_out,
@@ -310,7 +330,6 @@
     group_after,
     residual,
     smooth,
-    tables,
     applied_out,
     inverse_out,
     sums_out,
@@ -323,7 +342,7 @@
     sums = [None] * 4
     for t in range(TILES):
         window = slice(t * LANES, (t + 1) * LANES)
-        weight = tables[64 + t : 65 + t, :]
+        weight = lane_weights(t)
         applied = full[0][t]
         inverse = 1.0 / full[1][t]
         applied_out[:, window] = applied
@@ -402,7 +421,6 @@
         )
         geometry = geometry.reshape((3,) + flat)
         tables = jnp.asarray(lane_tables())
-        plane = jnp.asarray(plane_table())
 
         def bind(kernel):
             def body(*refs):
@@ -416,10 +434,15 @@
             bind(start_kernel),
             [flat, face_dev, face_dev, face_group, face_group],
             direction,
+        )
+        dev = both_ways(dev_low, dev_high, "dev")
+        diag, tables, plane = call(
+            bind(diagonal_kernel),
+            [flat, tables.shape, (LANES, 2 * LANES)],
+            geometry,
+            mass,
             tables,
         )
-        dev = both_ways(dev_low, dev_high, "dev")
-        (diag,) = call(bind(diagonal_kernel), [flat], geometry, mass, plane, tables)
         low, high = call(corners, [face_group] * 2, group_low, group_high, *dev)
         group = both_ways(low, high, "group")
         smooth, applied, dev_low, dev_high, group_low, group_high = call(
@@ -430,8 +453,8 @@
             *group,
             geometry,
             mass,
+            tables,
             plane,
-            tables,
             diag,
         )
         dev = both_ways(dev_low, dev_high, "dev")
@@ -439,18 +462,17 @@
         group = both_ways(low, high, "group")
         applied, inverse, sums = call(
             bind(products_kernel),
-            [flat, flat, (devs, 1, LANES)],
+            [flat, flat, (groups, 1, LANES)],
             applied,
             diag,
             *dev,
             *group,
             residual,
             smooth,
-            tables,
-        )
+        )
+        sums = lax.all_to_all(sums, "group", 0, 0)
+        (sums,) = call(middle_kernel, [(devs, 1, LANES)], sums)
         sums = lax.all_to_all(sums, "dev", 0, 0)
-        (sums,) = call(middle_kernel, [(groups, 1, LANES)], sums)
-        sums = lax.all_to_all(sums, "group", 0, 0)
         outs = call(
             final_kernel, [flat] * 3, sums, solution, residual, smooth, applied, inverse
         )

time: 84.8 us -> 81.7 us (0.963)
  local copies, waits for them, and re-layouts: 3.29 us -> 1.66 us
  blocking collectives: 35.4 us -> 34.2 us
  starting transfers between devices: 36.4 us -> 35.2 us
  waiting for transfers between devices: 5.58 us -> 6.47 us
    unnamed x18 -> x12, local copies, waits for them, and re-layouts: 3.29 us -> 1.66 us
    ppermute x4, starting transfers between devices: 10.8 us -> 9.69 us  [both_ways(): before = lax.ppermute(high, axis, up)]
    all_to_all x1, blocking collectives: 17 us -> 15.9 us  [on_device(): sums = lax.all_to_all(sums, 'group', 0, 0)]
    ppermute x4, waiting for transfers between devices: 4.86 us -> 5.75 us  [both_ways(): after = lax.ppermute(low, axis, [(j, i) for i, j in up])]
where the time goes in v2:
time: 81.7 us; the launch traced here: 81.2 us
  starting transfers between devices  35.2 us (43%)
  blocking collectives  34.2 us (42%)
  waiting for transfers between devices  6.47 us (8%)
  Pallas kernels  2.85 us (3%)
  local copies, waits for them, and re-layouts  1.66 us (2%)
    ppermute x4, starting transfers between devices, both_ways(): after = lax.ppermute(low, axis, [(j, i) for i, j in up])  25.5 us
    all_to_all x1, blocking collectives, on_device(): sums = lax.all_to_all(sums, 'dev', 0, 0)  18.3 us
    all_to_all x1, blocking collectives, on_device(): sums = lax.all_to_all(sums, 'group', 0, 0)  15.9 us
    ppermute x4, starting transfers between devices, both_ways(): before = lax.ppermute(high, axis, up)  9.69 us
    ppermute x4, waiting for transfers between devices, both_ways(): after = lax.ppermute(low, axis, [(j, i) for i, j in up])  5.75 us
    pallas_call x8, Pallas kernels, call(): pl.pallas_call(kernel, out_shape=outs, in_specs=[vmem] * len(args), out_s...  2.85 us
    unnamed x12, local copies, waits for them, and re-layouts  1.66 us
  transfers between devices with their start and end apart: 8, of which 5 were waited for; matrix products, arithmetic and copies ran while one was open for 0% of the time, Pallas kernels for 1%

profile of v2, /device:TPU:1, one launch (start us, length us, event | category | flops | bytes accessed | tf_op | source)
XLA Modules:
  0.0 81.2 jit_solution(4182942986664393857)
XLA Ops:
  0.6 0.0 copy-start
  0.6 0.0 copy-start.3
  0.7 0.9 %copy-done.3 = f32[1,2,16,512]{3,2,1,0:T(8,128)S(1)} copy-done((f32[1,2,16,512]{3,2,1,0:T(8,128)S(1)}, f32[1,2,16,512]{3,2,1,0:T(8,128)}, u32[]{:S(2)}) %copy-start.3) | copy-done | bytes 65560
  1.5 0.3 shard_map.85
  1.8 0.0 copy-start.2
  1.8 3.9 %collective-permute-start = (f32[16,128]{1,0:T(8,128)S(1)}, f32[16,128]{1,0:T(8,128)S(1)}, u32[]{:S(2)}, u32[]{:S(2)}) collective-permute-start(f32[16,128]{1,0:T(8,128)S(1)} %get-tuple-element.28), channel_id=1, source_target_pairs={{0,1},{1,2},{2,3},{3,4},{4,5},{5,6},{6,7},{7,8},{8,9},{9,10},{10,1... | collective-permute-start | bytes 24584 | tf_op jit(solution)/shard_map/ppermute | solution.py:402
  5.7 18.1 %collective-permute-start.1 = (f32[16,128]{1,0:T(8,128)S(1)}, f32[16,128]{1,0:T(8,128)S(1)}, u32[]{:S(2)}, u32[]{:S(2)}) collective-permute-start(f32[16,128]{1,0:T(8,128)S(1)} %get-tuple-element.29), channel_id=1, source_target_pairs={{1,0},{2,1},{3,2},{4,3},{5,4},{6,5},{7,6},{8,7},{9,8},{10,9},{11,1... | collective-permute-start | bytes 24584 | tf_op jit(solution)/shard_map/ppermute | solution.py:403
  23.9 0.0 collective-permute-done.refs_2_.refs_1_
  23.9 0.8 collective-permute-done.1.refs_3_.refs_2_
  24.7 0.1 shard_map.86
  24.7 2.8 %collective-permute-start.2 = (f32[32,128]{1,0:T(8,128)S(1)}, f32[32,128]{1,0:T(8,128)S(1)}, u32[]{:S(2)}, u32[]{:S(2)}) collective-permute-start(f32[32,128]{1,0:T(8,128)S(1)} %get-tuple-element.32), channel_id=1, source_target_pairs={{0,64},{64,128},{128,192},{192,256},{256,320},{320,384},{384,448},... | collective-permute-start | bytes 49160 | tf_op jit(solution)/shard_map/ppermute | solution.py:402
  27.6 0.0 collective-permute-start.3
  27.6 0.0 copy-done
  27.6 0.0 copy-done.2
  27.6 0.0 copy-start.5
  27.6 0.8 copy-done.5
  28.4 0.4 shard_map.87
  28.8 0.0 collective-permute-done.2.refs_3_
  28.8 1.9 %collective-permute-done.3.refs_4_ = f32[32,128]{1,0:T(8,128)S(1)} collective-permute-done((f32[32,128]{1,0:T(8,128)S(1)}, f32[32,128]{1,0:T(8,128)S(1)}, u32[]{:S(2)}, u32[]{:S(2)}) %collective-permute-start.3) | collective-permute-done | bytes 16416 | tf_op jit(solution)/shard_map/ppermute | solution.py:403
  30.7 0.9 %shard_map.88 = (f32[32,512]{1,0:T(8,128)S(1)}, f32[32,512]{1,0:T(8,128)S(1)}, f32[16,128]{1,0:T(8,128)S(1)}, f32[16,128]{1,0:T(8,128)S(1)}, f32[32,128]{1,0:T(8,128)S(1)}, /*index=5*/f32[32,128]{1,0:T(8,128)S(1)}) custom-call(f32[32,512]{1,0:T(8,128)S(1)} %get-tuple-element.27.refs_0_, f32[16,128]{1,0:T(8,128)S(1)} %collective-permute-done.refs_2_.refs_1_, ...), custom_call_target="tpu_custom_call" | custom-call | tf_op jit(solution)/shard_map/pallas_call | solution.py:390
  31.6 0.0 copy-start.1
  31.6 2.1 %collective-permute-start.4 = (f32[16,128]{1,0:T(8,128)S(1)}, f32[16,128]{1,0:T(8,128)S(1)}, u32[]{:S(2)}, u32[]{:S(2)}) collective-permute-start(f32[16,128]{1,0:T(8,128)S(1)} %get-tuple-element.38), channel_id=1, source_target_pairs={{0,1},{1,2},{2,3},{3,4},{4,5},{5,6},{6,7},{7,8},{8,9},{9,10},{10,1... | collective-permute-start | bytes 24584 | tf_op jit(solution)/shard_map/ppermute | solution.py:402
  33.7 7.2 %collective-permute-start.5 = (f32[16,128]{1,0:T(8,128)S(1)}, f32[16,128]{1,0:T(8,128)S(1)}, u32[]{:S(2)}, u32[]{:S(2)}) collective-permute-start(f32[16,128]{1,0:T(8,128)S(1)} %get-tuple-element.39), channel_id=1, source_target_pairs={{1,0},{2,1},{3,2},{4,3},{5,4},{6,5},{7,6},{8,7},{9,8},{10,9},{11,1... | collective-permute-start | bytes 24584 | tf_op jit(solution)/shard_map/ppermute | solution.py:403
  40.9 0.0 collective-permute-done.4.refs_2_
  41.0 0.8 collective-permute-done.5.refs_3_
  41.7 0.1 shard_map.89
  41.8 0.9 %collective-permute-start.6 = (f32[32,128]{1,0:T(8,128)S(1)}, f32[32,128]{1,0:T(8,128)S(1)}, u32[]{:S(2)}, u32[]{:S(2)}) collective-permute-start(f32[32,128]{1,0:T(8,128)S(1)} %get-tuple-element.42), channel_id=1, source_target_pairs={{0,64},{64,128},{128,192},{192,256},{256,320},{320,384},{384,448},... | collective-permute-start | bytes 49160 | tf_op jit(solution)/shard_map/ppermute | solution.py:402
  42.7 0.2 collective-permute-start.7
  42.8 0.7 collective-permute-done.6.refs_4_
  43.5 2.3 %collective-permute-done.7.refs_5_ = f32[32,128]{1,0:T(8,128)S(1)} collective-permute-done((f32[32,128]{1,0:T(8,128)S(1)}, f32[32,128]{1,0:T(8,128)S(1)}, u32[]{:S(2)}, u32[]{:S(2)}) %collective-permute-start.7) | collective-permute-done | bytes 16416 | tf_op jit(solution)/shard_map/ppermute | solution.py:403
  45.8 0.0 copy-done.1
  45.8 0.2 shard_map.90
  46.1 0.0 copy-start.4
  46.1 15.9 %all_to_all.10.parts = f32[16,1,128]{2,1,0:T(1,128)S(1)} all-to-all(f32[16,1,128]{2,1,0:T(1,128)S(1)} %get-tuple-element.45), channel_id=1, replica_groups=mesh['group'=16,'dev'=64] {'group'}, dimensions={0} | all-to-all | bytes 16384 | tf_op jit(solution)/shard_map/all_to_all | solution.py:473
  62.0 18.3 %all_to_all.11.parts = f32[64,1,128]{2,1,0:T(1,128)S(1)} all-to-all(f32[64,1,128]{2,1,0:T(1,128)S(1)} %shard_map.91), channel_id=1, replica_groups=mesh['group'=16,'dev'=64] {'dev'}, dimensions={0} | all-to-all | bytes 65536 | tf_op jit(solution)/shard_map/all_to_all | solution.py:475
  80.3 0.0 copy-done.4
  80.3 0.9 %shard_map.92 = (f32[32,512]{1,0:T(8,128)}, f32[32,512]{1,0:T(8,128)}, f32[32,512]{1,0:T(8,128)}) custom-call(f32[64,1,128]{2,1,0:T(1,128)S(1)} %all_to_all.11.parts, f32[32,512]{1,0:T(8,128)S(1)} %bitcast.15, f32[32,512]{1,0:T(8,128)S(1)} %bitcast.11, f32[32,512]{1,0:T(8,128)S(1)} %get-tuple-element.44.refs_7_.smooth, ...), custom_call_target="tpu_custom_call" | custom-call | tf_op jit(solution)/shard_map/pallas_call | solution.py:390
  (1 shorter events, 0.0 us)
Async XLA Ops:
  0.6 26.9 %copy-start = (bf16[3,1,2,16,512]{4,3,2,1,0:T(8,128)(2,1)S(1)}, bf16[3,1,2,16,512]{4,3,2,1,0:T(8,128)(2,1)}, u32[]{:S(2)}) copy-start(bf16[3,1,2,16,512]{4,3,2,1,0:T(8,128)(2,1)} %param.9) | copy-start | bytes 294916
  0.6 0.9 %copy-start.3 = (f32[1,2,16,512]{3,2,1,0:T(8,128)S(1)}, f32[1,2,16,512]{3,2,1,0:T(8,128)}, u32[]{:S(2)}) copy-start(f32[1,2,16,512]{3,2,1,0:T(8,128)} %param.8) | copy-start | bytes 196612
  1.8 25.8 %copy-start.2 = (bf16[1,2,16,512]{3,2,1,0:T(8,128)(2,1)S(1)}, bf16[1,2,16,512]{3,2,1,0:T(8,128)(2,1)}, u32[]{:S(2)}) copy-start(bf16[1,2,16,512]{3,2,1,0:T(8,128)(2,1)} %param.10) | copy-start | bytes 98308
  1.8 22.1 %collective-permute-start = (f32[16,128]{1,0:T(8,128)S(1)}, f32[16,128]{1,0:T(8,128)S(1)}, u32[]{:S(2)}, u32[]{:S(2)}) collective-permute-start(f32[16,128]{1,0:T(8,128)S(1)} %get-tuple-element.28), channel_id=1, source_target_pairs={{0,1},{1,2},{2,3},{3,4},{4,5},{5,6},{6,7},{7,8},{8,9},{9,10},{10,1... | collective-permute-start | bytes 24584 | tf_op jit(solution)/shard_map/ppermute | solution.py:402
  5.7 18.9 %collective-permute-start.1 = (f32[16,128]{1,0:T(8,128)S(1)}, f32[16,128]{1,0:T(8,128)S(1)}, u32[]{:S(2)}, u32[]{:S(2)}) collective-permute-start(f32[16,128]{1,0:T(8,128)S(1)} %get-tuple-element.29), channel_id=1, source_target_pairs={{1,0},{2,1},{3,2},{4,3},{5,4},{6,5},{7,6},{8,7},{9,8},{10,9},{11,1... | collective-permute-start | bytes 24584 | tf_op jit(solution)/shard_map/ppermute | solution.py:403
  24.7 4.0 %collective-permute-start.2 = (f32[32,128]{1,0:T(8,128)S(1)}, f32[32,128]{1,0:T(8,128)S(1)}, u32[]{:S(2)}, u32[]{:S(2)}) collective-permute-start(f32[32,128]{1,0:T(8,128)S(1)} %get-tuple-element.32), channel_id=1, source_target_pairs={{0,64},{64,128},{128,192},{192,256},{256,320},{320,384},{384,448},... | collective-permute-start | bytes 49160 | tf_op jit(solution)/shard_map/ppermute | solution.py:402
  27.6 3.2 %collective-permute-start.3 = (f32[32,128]{1,0:T(8,128)S(1)}, f32[32,128]{1,0:T(8,128)S(1)}, u32[]{:S(2)}, u32[]{:S(2)}) collective-permute-start(f32[32,128]{1,0:T(8,128)S(1)} %get-tuple-element.33), channel_id=1, source_target_pairs={{64,0},{128,64},{192,128},{256,192},{320,256},{384,320},{448,384},... | collective-permute-start | bytes 49160 | tf_op jit(solution)/shard_map/ppermute | solution.py:403
  27.6 0.8 copy-start.5
  31.6 14.2 %copy-start.1 = (f32[1,2,16,512]{3,2,1,0:T(8,128)S(1)}, f32[1,2,16,512]{3,2,1,0:T(8,128)}, u32[]{:S(2)}) copy-start(f32[1,2,16,512]{3,2,1,0:T(8,128)} %param.7) | copy-start | bytes 196612
  31.6 9.3 %collective-permute-start.4 = (f32[16,128]{1,0:T(8,128)S(1)}, f32[16,128]{1,0:T(8,128)S(1)}, u32[]{:S(2)}, u32[]{:S(2)}) collective-permute-start(f32[16,128]{1,0:T(8,128)S(1)} %get-tuple-element.38), channel_id=1, source_target_pairs={{0,1},{1,2},{2,3},{3,4},{4,5},{5,6},{6,7},{7,8},{8,9},{9,10},{10,1... | collective-permute-start | bytes 24584 | tf_op jit(solution)/shard_map/ppermute | solution.py:402
  33.7 8.0 %collective-permute-start.5 = (f32[16,128]{1,0:T(8,128)S(1)}, f32[16,128]{1,0:T(8,128)S(1)}, u32[]{:S(2)}, u32[]{:S(2)}) collective-permute-start(f32[16,128]{1,0:T(8,128)S(1)} %get-tuple-element.39), channel_id=1, source_target_pairs={{1,0},{2,1},{3,2},{4,3},{5,4},{6,5},{7,6},{8,7},{9,8},{10,9},{11,1... | collective-permute-start | bytes 24584 | tf_op jit(solution)/shard_map/ppermute | solution.py:403
  41.8 1.7 %collective-permute-start.6 = (f32[32,128]{1,0:T(8,128)S(1)}, f32[32,128]{1,0:T(8,128)S(1)}, u32[]{:S(2)}, u32[]{:S(2)}) collective-permute-start(f32[32,128]{1,0:T(8,128)S(1)} %get-tuple-element.42), channel_id=1, source_target_pairs={{0,64},{64,128},{128,192},{192,256},{256,320},{320,384},{384,448},... | collective-permute-start | bytes 49160 | tf_op jit(solution)/shard_map/ppermute | solution.py:402
  42.7 3.2 %collective-permute-start.7 = (f32[32,128]{1,0:T(8,128)S(1)}, f32[32,128]{1,0:T(8,128)S(1)}, u32[]{:S(2)}, u32[]{:S(2)}) collective-permute-start(f32[32,128]{1,0:T(8,128)S(1)} %get-tuple-element.43), channel_id=1, source_target_pairs={{64,0},{128,64},{192,128},{256,192},{320,256},{384,320},{448,384},... | collective-permute-start | bytes 49160 | tf_op jit(solution)/shard_map/ppermute | solution.py:403
  46.1 34.3 %copy-start.4 = (f32[1,2,16,512]{3,2,1,0:T(8,128)S(1)}, f32[1,2,16,512]{3,2,1,0:T(8,128)}, u32[]{:S(2)}) copy-start(f32[1,2,16,512]{3,2,1,0:T(8,128)} %param.6) | copy-start | bytes 196612

commit v3 on v2

--- a/solution.py
+++ b/solution.py
@@ -11,6 +11,7 @@
 TILES = NP**3 // LANES
 HALF = NP * NP
 SECOND = 64
+VMEM_BYTES = 8 * 2**20
 
 lobatto_nodes = [
     -1.0,
@@ -197,24 +198,19 @@
     return out
 
 
-def matmul(left, right):
-    return lax.dot_general(
-        left,
-        right,
-        (((1,), (0,)), ((), ())),
-        precision=lax.Precision.HIGHEST,
-        preferred_element_type=jnp.float32,
-    )
-
-
-def matmul_t(left, right):
-    return lax.dot_general(
-        left,
-        right,
-        (((1,), (1,)), ((), ())),
-        precision=lax.Precision.HIGHEST,
-        preferred_element_type=jnp.float32,
-    )
+def halves(value):
+    high = value.astype(jnp.bfloat16)
+    return high, (value - high.astype(jnp.float32)).astype(jnp.bfloat16)
+
+
+def matmul(lefts, rights, transposed=False):
+    dims = (((1,), (1 if transposed else 0,)), ((), ()))
+    total = None
+    for n, left in enumerate(lefts):
+        for right in rights[: len(rights) - n]:
+            term = lax.dot_general(left, right, dims, preferred_element_type=jnp.float32)
+            total = term if total is None else total + term
+    return total
 
 
 def tiles_of(value):
@@ -247,35 +243,34 @@
     group_high[...] = pack_group([blocks], True)
 
 
-def diagonal_kernel(dims, geometry, mass, tables, diag_out, tables_out, plane_out):
-    geo = [tiles_of(geometry[c].astype(jnp.float32)) for c in range(3)]
-    first = first_direction(tables, 32, geo[0], squared=True)
+def diagonal_kernel(dims, geometry, mass, tables, diag_out, tables_out, high_out, low_out):
+    first = first_direction(
+        tables, 32, tiles_of(geometry[0].astype(jnp.float32)), squared=True
+    )
     table = plane_table(tables)
     tables_out[...] = tables[...]
-    plane_out[...] = table
-    pair = jnp.concatenate([stack_rows(geo[1]), stack_rows(geo[2])], axis=1)
-    rest = unstack_rows(matmul_t(pair, table * table))
+    high_out[...], low_out[...] = halves(table)
+    pair = jnp.concatenate(
+        [stack_rows(tiles_of(geometry[1])), stack_rows(tiles_of(geometry[2]))], axis=1
+    )
+    rest = unstack_rows(matmul([pair], halves(table * table), transposed=True))
     masses = tiles_of(mass[...].astype(jnp.float32))
     local = [a + b + c for a, b, c in zip(first, rest, masses)]
     diag_out[...] = join(local_assemble(blocks_of(local, dims)))
 
 
-def corner_kernel(dims, group_low, group_high, before, after, low_out, high_out):
+def corner_kernel(dims, dev_low, dev_high, before, after, low_out, high_out):
     eb, ez = dims
-    low_recv = before[...]
-    high_recv = after[...]
-    lane = lanes(ez)
-    j = (lane // NP) % NP
-    for ref, out, upper in ((group_low, low_out, False), (group_high, high_out, True)):
-        shift_low = NP - HALF if upper else 0
-        shift_high = 0 if upper else HALF - NP
-        blocks = [ref[b * ez : (b + 1) * ez, :] for b in range(eb)]
-        low = roll(low_recv, shift_low, 1) if shift_low else low_recv
-        high = roll(high_recv, shift_high, 1) if shift_high else high_recv
-        blocks[0] = blocks[0] + jnp.where(j == 0, low, 0.0)
-        blocks[-1] = blocks[-1] + jnp.where(j == NP - 1, high, 0.0)
-        for b in range(eb):
-            out[b * ez : (b + 1) * ez, :] = blocks[b]
+    i = (lanes(ez) // NP) % NP
+    for ref, out, upper in ((dev_low, low_out, False), (dev_high, high_out, True)):
+        start = (eb - 1) * ez if upper else 0
+        low = before[start : start + ez, :]
+        high = after[start : start + ez, :]
+        if upper:
+            low = roll(low, NP - HALF, 1)
+        else:
+            high = roll(high, HALF - NP, 1)
+        out[...] = ref[...] + jnp.where(i == 0, low, jnp.where(i == NP - 1, high, 0.0))
 
 
 def operator_kernel(
@@ -288,7 +283,8 @@
     geometry,
     mass,
     tables,
-    plane,
+    plane_high,
+    plane_low,
     diag,
     smooth_out,
     applied_out,
@@ -303,11 +299,11 @@
     smooth_out[...] = join(blocks)
     tiles = [jnp.concatenate(tile, axis=0) for tile in blocks]
     geo = [tiles_of(geometry[c].astype(jnp.float32)) for c in range(3)]
-    table = plane[...]
+    table = (plane_high[...], plane_low[...])
     first = [g * f for g, f in zip(geo[0], first_direction(tables, 0, tiles))]
-    gradient = matmul(stack_rows(tiles), table)
+    gradient = matmul(halves(stack_rows(tiles)), table)
     pair = jnp.concatenate([stack_rows(geo[1]), stack_rows(geo[2])], axis=1) * gradient
-    rest = unstack_rows(matmul_t(pair, table))
+    rest = unstack_rows(matmul(halves(pair), table, transposed=True))
     first = first_direction(tables, 32, first)
     masses = tiles_of(mass[...].astype(jnp.float32))
     local = [a + b + m * u for a, b, m, u in zip(first, rest, masses, tiles)]
@@ -369,30 +365,38 @@
     sums_out[...] = jnp.broadcast_to(total, sums_out.shape)
 
 
-def final_kernel(
-    parts, solution, residual, smooth, applied, inverse, solution_out, residual_out, direction_out
-):
+def final_kernel(parts, solution, residual, smooth, applied, inverse, *refs):
+    targets, buffers, sems = refs[:3], refs[3:6], refs[6]
+    copies = [
+        pltpu.make_async_copy(source, target, sems.at[n])
+        for n, (source, target) in enumerate(zip(buffers, targets))
+    ]
     total = jnp.sum(parts[...], axis=0)
     norm_now, curvature, cross, quad = (total[:, n : n + 1] for n in range(4))
     step = norm_now / curvature
+    direction = smooth[...]
+    buffers[0][...] = solution[...] + step * direction
+    copies[0].start()
+    res = residual[...] - step * applied[...]
+    buffers[1][...] = res
+    copies[1].start()
     norm_next = norm_now - 2.0 * step * cross + step * step * quad
-    ratio = norm_next / norm_now
-    direction = smooth[...]
-    res = residual[...] - step * applied[...]
-    solution_out[...] = solution[...] + step * direction
-    residual_out[...] = res
-    direction_out[...] = res * inverse[...] + ratio * direction
+    buffers[2][...] = res * inverse[...] + (norm_next / norm_now) * direction
+    copies[2].start()
+    for copy in copies:
+        copy.wait()
 
 
 def call(kernel, shapes, *args):
-    outs = tuple(jax.ShapeDtypeStruct(shape, jnp.float32) for shape in shapes)
+    typed = [s if isinstance(s[1], type) else (s, jnp.float32) for s in shapes]
+    outs = tuple(jax.ShapeDtypeStruct(shape, dtype) for shape, dtype in typed)
     vmem = pl.BlockSpec(memory_space=pltpu.VMEM)
     return pl.pallas_call(
         kernel,
         out_shape=outs,
         in_specs=[vmem] * len(args),
         out_specs=(vmem,) * len(outs),
-        compiler_params=pltpu.CompilerParams(vmem_limit_bytes=8 * 2**20),
+        compiler_params=pltpu.CompilerParams(vmem_limit_bytes=VMEM_BYTES),
     )(*args)
 
 
@@ -429,22 +433,24 @@
             body.__name__ = kernel.__name__
             return body
 
-        corners = bind(corner_kernel)
+        def exchange(dev_low, dev_high, group_low, group_high):
+            group = both_ways(group_low, group_high, "group")
+            faces = call(bind(corner_kernel), [face_dev] * 2, dev_low, dev_high, *group)
+            return both_ways(*faces, "dev"), group
+
         field, dev_low, dev_high, group_low, group_high = call(
             bind(start_kernel),
             [flat, face_dev, face_dev, face_group, face_group],
             direction,
         )
-        dev = both_ways(dev_low, dev_high, "dev")
-        diag, tables, plane = call(
+        diag, tables, *plane = call(
             bind(diagonal_kernel),
-            [flat, tables.shape, (LANES, 2 * LANES)],
+            [flat, tables.shape] + [((LANES, 2 * LANES), jnp.bfloat16)] * 2,
             geometry,
             mass,
             tables,
         )
-        low, high = call(corners, [face_group] * 2, group_low, group_high, *dev)
-        group = both_ways(low, high, "group")
+        dev, group = exchange(dev_low, dev_high, group_low, group_high)
         smooth, applied, dev_low, dev_high, group_low, group_high = call(
             bind(operator_kernel),
             [flat, flat, face_dev, face_dev, face_group, face_group],
@@ -454,12 +460,10 @@
             geometry,
             mass,
             tables,
-            plane,
+            *plane,
             diag,
         )
-        dev = both_ways(dev_low, dev_high, "dev")
-        low, high = call(corners, [face_group] * 2, group_low, group_high, *dev)
-        group = both_ways(low, high, "group")
+        dev, group = exchange(dev_low, dev_high, group_low, group_high)
         applied, inverse, sums = call(
             bind(products_kernel),
             [flat, flat, (groups, 1, LANES)],
@@ -473,9 +477,14 @@
         sums = lax.all_to_all(sums, "group", 0, 0)
         (sums,) = call(middle_kernel, [(devs, 1, LANES)], sums)
         sums = lax.all_to_all(sums, "dev", 0, 0)
-        outs = call(
-            final_kernel, [flat] * 3, sums, solution, residual, smooth, applied, inverse
-        )
+        outs = pl.pallas_call(
+            final_kernel,
+            out_shape=(jax.ShapeDtypeStruct(flat, jnp.float32),) * 3,
+            in_specs=[pl.BlockSpec(memory_space=pltpu.VMEM)] * 6,
+            out_specs=(pl.BlockSpec(memory_space=pltpu.HBM),) * 3,
+            scratch_shapes=[pltpu.VMEM(flat, jnp.float32)] * 3 + [pltpu.SemaphoreType.DMA((3,))],
+            compiler_params=pltpu.CompilerParams(vmem_limit_bytes=VMEM_BYTES),
+        )(sums, solution, residual, smooth, applied, inverse)
         return tuple(out.reshape(local) for out in outs)
 
     spec = P("group", "dev", None, None)

time: 81.7 us -> 81.1 us (level)
  waiting for transfers between devices: 6.47 us -> 4.06 us
  starting transfers between devices: 35.2 us -> 36.7 us
    ppermute x4, starting transfers between devices: 25.5 us -> 29.9 us  [both_ways(): after = lax.ppermute(low, axis, [(j, i) for i, j in up])]
    ppermute x4, waiting for transfers between devices: 5.75 us -> 2.74 us  [both_ways(): after = lax.ppermute(low, axis, [(j, i) for i, j in up])]
    ppermute x4, starting transfers between devices: 9.69 us -> 6.83 us  [both_ways(): before = lax.ppermute(high, axis, up)]
    pallas_call x8 -> x7, Pallas kernels: 2.85 us -> 1.72 us  [call(): pl.pallas_call(kernel, out_shape=outs, in_specs=[vmem] * len(args), out_s...]
    pallas_call x0 -> x1, Pallas kernels: none -> 0.88 us  [on_device(): pl.pallas_call(final_kernel, out_shape=(jax.ShapeDtypeStruct(flat, jnp.fl...]
  transfers between devices with their start and end apart: 8 -> 8, of which waited for: 5 -> 5; matrix products, arithmetic and copies ran while one was open for 0% -> 0% of each run, Pallas kernels for 1% -> 0%
where the time goes in v3:
time: 81.1 us; the launch traced here: 80.6 us
  starting transfers between devices  36.7 us (45%)
  blocking collectives  34.8 us (43%)
  waiting for transfers between devices  4.06 us (5%)
  Pallas kernels  2.61 us (3%)
  local copies, waits for them, and re-layouts  1.66 us (2%)
    ppermute x4, starting transfers between devices, both_ways(): after = lax.ppermute(low, axis, [(j, i) for i, j in up])  29.9 us
    all_to_all x1, blocking collectives, on_device(): sums = lax.all_to_all(sums, 'dev', 0, 0)  18.3 us
    all_to_all x1, blocking collectives, on_device(): sums = lax.all_to_all(sums, 'group', 0, 0)  16.5 us
    ppermute x4, starting transfers between devices, both_ways(): before = lax.ppermute(high, axis, up)  6.83 us
    ppermute x4, waiting for transfers between devices, both_ways(): after = lax.ppermute(low, axis, [(j, i) for i, j in up])  2.74 us
    pallas_call x7, Pallas kernels, call(): pl.pallas_call(kernel, out_shape=outs, in_specs=[vmem] * len(args), out_s...  1.72 us
    unnamed x12, local copies, waits for them, and re-layouts  1.66 us
  transfers between devices with their start and end apart: 8, of which 5 were waited for; matrix products, arithmetic and copies ran while one was open for 0% of the time, Pallas kernels for 0%

profile of v3, /device:TPU:1, one launch (start us, length us, event | category | flops | bytes accessed | tf_op | source)
XLA Modules:
  0.0 80.6 jit_solution(7019662845365185599)
XLA Ops:
  0.6 0.0 copy-start
  0.6 0.0 copy-start.3
  0.7 0.9 %copy-done.3 = f32[1,2,16,512]{3,2,1,0:T(8,128)S(1)} copy-done((f32[1,2,16,512]{3,2,1,0:T(8,128)S(1)}, f32[1,2,16,512]{3,2,1,0:T(8,128)}, u32[]{:S(2)}) %copy-start.3) | copy-done | bytes 65560
  1.5 0.3 shard_map.85
  1.8 0.0 copy-start.2
  1.8 2.8 %collective-permute-start = (f32[32,128]{1,0:T(8,128)S(1)}, f32[32,128]{1,0:T(8,128)S(1)}, u32[]{:S(2)}, u32[]{:S(2)}) collective-permute-start(f32[32,128]{1,0:T(8,128)S(1)} %get-tuple-element.31), channel_id=1, source_target_pairs={{0,64},{64,128},{128,192},{192,256},{256,320},{320,384},{384,448},... | collective-permute-start | bytes 49160 | tf_op jit(solution)/shard_map/ppermute | solution.py:406
  4.6 11.4 %collective-permute-start.1 = (f32[32,128]{1,0:T(8,128)S(1)}, f32[32,128]{1,0:T(8,128)S(1)}, u32[]{:S(2)}, u32[]{:S(2)}) collective-permute-start(f32[32,128]{1,0:T(8,128)S(1)} %get-tuple-element.32), channel_id=1, source_target_pairs={{64,0},{128,64},{192,128},{256,192},{320,256},{384,320},{448,384},... | collective-permute-start | bytes 49160 | tf_op jit(solution)/shard_map/ppermute | solution.py:407
  15.9 0.7 collective-permute-done.refs_2_.refs_3_
  16.6 0.2 collective-permute-done.1.refs_3_.refs_4_
  16.8 0.1 shard_map.86
  16.9 1.9 %collective-permute-start.2 = (f32[16,128]{1,0:T(8,128)S(1)}, f32[16,128]{1,0:T(8,128)S(1)}, u32[]{:S(2)}, u32[]{:S(2)}) collective-permute-start(f32[16,128]{1,0:T(8,128)S(1)} %get-tuple-element.33), channel_id=1, source_target_pairs={{0,1},{1,2},{2,3},{3,4},{4,5},{5,6},{6,7},{7,8},{8,9},{9,10},{10,1... | collective-permute-start | bytes 24584 | tf_op jit(solution)/shard_map/ppermute | solution.py:406
  18.8 10.6 %collective-permute-start.3 = (f32[16,128]{1,0:T(8,128)S(1)}, f32[16,128]{1,0:T(8,128)S(1)}, u32[]{:S(2)}, u32[]{:S(2)}) collective-permute-start(f32[16,128]{1,0:T(8,128)S(1)} %get-tuple-element.34), channel_id=1, source_target_pairs={{1,0},{2,1},{3,2},{4,3},{5,4},{6,5},{7,6},{8,7},{9,8},{10,9},{11,1... | collective-permute-start | bytes 24584 | tf_op jit(solution)/shard_map/ppermute | solution.py:407
  29.4 0.0 copy-done
  29.4 0.0 copy-done.2
  29.4 0.0 copy-start.5
  29.4 0.8 copy-done.5
  30.2 0.3 shard_map.87
  30.5 0.0 collective-permute-done.2.refs_1_
  30.5 0.0 collective-permute-done.3.refs_2_
  30.5 0.7 shard_map.88
  31.3 0.0 copy-start.1
  31.3 0.2 collective-permute-start.4
  31.5 0.7 collective-permute-start.5
  32.2 0.7 collective-permute-done.4.refs_2_.refs_4_
  32.9 1.8 %collective-permute-done.5.refs_3_.refs_5_ = f32[32,128]{1,0:T(8,128)S(1)} collective-permute-done((f32[32,128]{1,0:T(8,128)S(1)}, f32[32,128]{1,0:T(8,128)S(1)}, u32[]{:S(2)}, u32[]{:S(2)}) %collective-permute-start.5) | collective-permute-done | bytes 16416 | tf_op jit(solution)/shard_map/ppermute | solution.py:407
  34.6 0.1 shard_map.89
  34.7 1.9 %collective-permute-start.6 = (f32[16,128]{1,0:T(8,128)S(1)}, f32[16,128]{1,0:T(8,128)S(1)}, u32[]{:S(2)}, u32[]{:S(2)}) collective-permute-start(f32[16,128]{1,0:T(8,128)S(1)} %get-tuple-element.44), channel_id=1, source_target_pairs={{0,1},{1,2},{2,3},{3,4},{4,5},{5,6},{6,7},{7,8},{8,9},{9,10},{10,1... | collective-permute-start | bytes 24584 | tf_op jit(solution)/shard_map/ppermute | solution.py:406
  36.6 7.2 %collective-permute-start.7 = (f32[16,128]{1,0:T(8,128)S(1)}, f32[16,128]{1,0:T(8,128)S(1)}, u32[]{:S(2)}, u32[]{:S(2)}) collective-permute-start(f32[16,128]{1,0:T(8,128)S(1)} %get-tuple-element.45), channel_id=1, source_target_pairs={{1,0},{2,1},{3,2},{4,3},{5,4},{6,5},{7,6},{8,7},{9,8},{10,9},{11,1... | collective-permute-start | bytes 24584 | tf_op jit(solution)/shard_map/ppermute | solution.py:407
  43.9 0.0 collective-permute-done.6.refs_2_
  43.9 0.8 collective-permute-done.7.refs_3_
  44.7 0.0 copy-done.1
  44.7 0.2 shard_map.90
  44.9 0.0 copy-start.4
  44.9 16.5 %all_to_all.10.parts = f32[16,1,128]{2,1,0:T(1,128)S(1)} all-to-all(f32[16,1,128]{2,1,0:T(1,128)S(1)} %get-tuple-element.47), channel_id=1, replica_groups=mesh['group'=16,'dev'=64] {'group'}, dimensions={0} | all-to-all | bytes 16384 | tf_op jit(solution)/shard_map/all_to_all | solution.py:477
  61.5 18.3 %all_to_all.11.parts = f32[64,1,128]{2,1,0:T(1,128)S(1)} all-to-all(f32[64,1,128]{2,1,0:T(1,128)S(1)} %shard_map.91), channel_id=1, replica_groups=mesh['group'=16,'dev'=64] {'dev'}, dimensions={0} | all-to-all | bytes 65536 | tf_op jit(solution)/shard_map/all_to_all | solution.py:479
  79.7 0.0 copy-done.4
  79.7 0.9 %shard_map.92 = (f32[32,512]{1,0:T(8,128)}, f32[32,512]{1,0:T(8,128)}, f32[32,512]{1,0:T(8,128)}) custom-call(f32[64,1,128]{2,1,0:T(1,128)S(1)} %all_to_all.11.parts, f32[32,512]{1,0:T(8,128)S(1)} %bitcast.15, f32[32,512]{1,0:T(8,128)S(1)} %bitcast.11, f32[32,512]{1,0:T(8,128)S(1)} %get-tuple-element.46.refs_7_.smooth, ...), custom_call_target="tpu_custom_call" | custom-call | tf_op jit(solution)/shard_map/pallas_call | solution.py:480
  (1 shorter events, 0.0 us)
Async XLA Ops:
  0.6 28.7 %copy-start = (bf16[3,1,2,16,512]{4,3,2,1,0:T(8,128)(2,1)S(1)}, bf16[3,1,2,16,512]{4,3,2,1,0:T(8,128)(2,1)}, u32[]{:S(2)}) copy-start(bf16[3,1,2,16,512]{4,3,2,1,0:T(8,128)(2,1)} %param.9) | copy-start | bytes 294916
  0.6 0.9 %copy-start.3 = (f32[1,2,16,512]{3,2,1,0:T(8,128)S(1)}, f32[1,2,16,512]{3,2,1,0:T(8,128)}, u32[]{:S(2)}) copy-start(f32[1,2,16,512]{3,2,1,0:T(8,128)} %param.8) | copy-start | bytes 196612
  1.8 27.6 %copy-start.2 = (bf16[1,2,16,512]{3,2,1,0:T(8,128)(2,1)S(1)}, bf16[1,2,16,512]{3,2,1,0:T(8,128)(2,1)}, u32[]{:S(2)}) copy-start(bf16[1,2,16,512]{3,2,1,0:T(8,128)(2,1)} %param.10) | copy-start | bytes 98308
  1.8 14.8 %collective-permute-start = (f32[32,128]{1,0:T(8,128)S(1)}, f32[32,128]{1,0:T(8,128)S(1)}, u32[]{:S(2)}, u32[]{:S(2)}) collective-permute-start(f32[32,128]{1,0:T(8,128)S(1)} %get-tuple-element.31), channel_id=1, source_target_pairs={{0,64},{64,128},{128,192},{192,256},{256,320},{320,384},{384,448},... | collective-permute-start | bytes 49160 | tf_op jit(solution)/shard_map/ppermute | solution.py:406
  4.6 12.2 %collective-permute-start.1 = (f32[32,128]{1,0:T(8,128)S(1)}, f32[32,128]{1,0:T(8,128)S(1)}, u32[]{:S(2)}, u32[]{:S(2)}) collective-permute-start(f32[32,128]{1,0:T(8,128)S(1)} %get-tuple-element.32), channel_id=1, source_target_pairs={{64,0},{128,64},{192,128},{256,192},{320,256},{384,320},{448,384},... | collective-permute-start | bytes 49160 | tf_op jit(solution)/shard_map/ppermute | solution.py:407
  16.9 13.7 %collective-permute-start.2 = (f32[16,128]{1,0:T(8,128)S(1)}, f32[16,128]{1,0:T(8,128)S(1)}, u32[]{:S(2)}, u32[]{:S(2)}) collective-permute-start(f32[16,128]{1,0:T(8,128)S(1)} %get-tuple-element.33), channel_id=1, source_target_pairs={{0,1},{1,2},{2,3},{3,4},{4,5},{5,6},{6,7},{7,8},{8,9},{9,10},{10,1... | collective-permute-start | bytes 24584 | tf_op jit(solution)/shard_map/ppermute | solution.py:406
  18.8 11.8 %collective-permute-start.3 = (f32[16,128]{1,0:T(8,128)S(1)}, f32[16,128]{1,0:T(8,128)S(1)}, u32[]{:S(2)}, u32[]{:S(2)}) collective-permute-start(f32[16,128]{1,0:T(8,128)S(1)} %get-tuple-element.34), channel_id=1, source_target_pairs={{1,0},{2,1},{3,2},{4,3},{5,4},{6,5},{7,6},{8,7},{9,8},{10,9},{11,1... | collective-permute-start | bytes 24584 | tf_op jit(solution)/shard_map/ppermute | solution.py:407
  29.4 0.8 copy-start.5
  31.3 13.4 %copy-start.1 = (f32[1,2,16,512]{3,2,1,0:T(8,128)S(1)}, f32[1,2,16,512]{3,2,1,0:T(8,128)}, u32[]{:S(2)}) copy-start(f32[1,2,16,512]{3,2,1,0:T(8,128)} %param.7) | copy-start | bytes 196612
  31.3 1.6 %collective-permute-start.4 = (f32[32,128]{1,0:T(8,128)S(1)}, f32[32,128]{1,0:T(8,128)S(1)}, u32[]{:S(2)}, u32[]{:S(2)}) collective-permute-start(f32[32,128]{1,0:T(8,128)S(1)} %get-tuple-element.42), channel_id=1, source_target_pairs={{0,64},{64,128},{128,192},{192,256},{256,320},{320,384},{384,448},... | collective-permute-start | bytes 49160 | tf_op jit(solution)/shard_map/ppermute | solution.py:406
  31.5 3.2 %collective-permute-start.5 = (f32[32,128]{1,0:T(8,128)S(1)}, f32[32,128]{1,0:T(8,128)S(1)}, u32[]{:S(2)}, u32[]{:S(2)}) collective-permute-start(f32[32,128]{1,0:T(8,128)S(1)} %get-tuple-element.43), channel_id=1, source_target_pairs={{64,0},{128,64},{192,128},{256,192},{320,256},{384,320},{448,384},... | collective-permute-start | bytes 49160 | tf_op jit(solution)/shard_map/ppermute | solution.py:407
  34.7 9.2 %collective-permute-start.6 = (f32[16,128]{1,0:T(8,128)S(1)}, f32[16,128]{1,0:T(8,128)S(1)}, u32[]{:S(2)}, u32[]{:S(2)}) collective-permute-start(f32[16,128]{1,0:T(8,128)S(1)} %get-tuple-element.44), channel_id=1, source_target_pairs={{0,1},{1,2},{2,3},{3,4},{4,5},{5,6},{6,7},{7,8},{8,9},{9,10},{10,1... | collective-permute-start | bytes 24584 | tf_op jit(solution)/shard_map/ppermute | solution.py:406
  36.6 8.0 %collective-permute-start.7 = (f32[16,128]{1,0:T(8,128)S(1)}, f32[16,128]{1,0:T(8,128)S(1)}, u32[]{:S(2)}, u32[]{:S(2)}) collective-permute-start(f32[16,128]{1,0:T(8,128)S(1)} %get-tuple-element.45), channel_id=1, source_target_pairs={{1,0},{2,1},{3,2},{4,3},{5,4},{6,5},{7,6},{8,7},{9,8},{10,9},{11,1... | collective-permute-start | bytes 24584 | tf_op jit(solution)/shard_map/ppermute | solution.py:407
  44.9 34.9 %copy-start.4 = (f32[1,2,16,512]{3,2,1,0:T(8,128)S(1)}, f32[1,2,16,512]{3,2,1,0:T(8,128)}, u32[]{:S(2)}) copy-start(f32[1,2,16,512]{3,2,1,0:T(8,128)} %param.6) | copy-start | bytes 196612

commit v4 on v3

--- a/solution.py
+++ b/solution.py
@@ -259,7 +259,7 @@
     diag_out[...] = join(local_assemble(blocks_of(local, dims)))
 
 
-def corner_kernel(dims, dev_low, dev_high, before, after, low_out, high_out):
+def corner_kernel(dims, dev_low, dev_high, before, after, ready, low_out, high_out):
     eb, ez = dims
     i = (lanes(ez) // NP) % NP
     for ref, out, upper in ((dev_low, low_out, False), (dev_high, high_out, True)):
@@ -365,26 +365,19 @@
     sums_out[...] = jnp.broadcast_to(total, sums_out.shape)
 
 
-def final_kernel(parts, solution, residual, smooth, applied, inverse, *refs):
-    targets, buffers, sems = refs[:3], refs[3:6], refs[6]
-    copies = [
-        pltpu.make_async_copy(source, target, sems.at[n])
-        for n, (source, target) in enumerate(zip(buffers, targets))
-    ]
+def final_kernel(
+    parts, solution, residual, smooth, applied, inverse, solution_out, residual_out, direction_out
+):
     total = jnp.sum(parts[...], axis=0)
     norm_now, curvature, cross, quad = (total[:, n : n + 1] for n in range(4))
     step = norm_now / curvature
+    norm_next = norm_now - 2.0 * step * cross + step * step * quad
+    ratio = norm_next / norm_now
     direction = smooth[...]
-    buffers[0][...] = solution[...] + step * direction
-    copies[0].start()
     res = residual[...] - step * applied[...]
-    buffers[1][...] = res
-    copies[1].start()
-    norm_next = norm_now - 2.0 * step * cross + step * step * quad
-    buffers[2][...] = res * inverse[...] + (norm_next / norm_now) * direction
-    copies[2].start()
-    for copy in copies:
-        copy.wait()
+    solution_out[...] = solution[...] + step * direction
+    residual_out[...] = res
+    direction_out[...] = res * inverse[...] + ratio * direction
 
 
 def call(kernel, shapes, *args):
@@ -433,9 +426,11 @@
             body.__name__ = kernel.__name__
             return body
 
-        def exchange(dev_low, dev_high, group_low, group_high):
+        def exchange(dev_low, dev_high, group_low, group_high, ready):
             group = both_ways(group_low, group_high, "group")
-            faces = call(bind(corner_kernel), [face_dev] * 2, dev_low, dev_high, *group)
+            faces = call(
+                bind(corner_kernel), [face_dev] * 2, dev_low, dev_high, *group, ready
+            )
             return both_ways(*faces, "dev"), group
 
         field, dev_low, dev_high, group_low, group_high = call(
@@ -450,7 +445,7 @@
             mass,
             tables,
         )
-        dev, group = exchange(dev_low, dev_high, group_low, group_high)
+        dev, group = exchange(dev_low, dev_high, group_low, group_high, tables)
         smooth, applied, dev_low, dev_high, group_low, group_high = call(
             bind(operator_kernel),
             [flat, flat, face_dev, face_dev, face_group, face_group],
@@ -463,7 +458,7 @@
             *plane,
             diag,
         )
-        dev, group = exchange(dev_low, dev_high, group_low, group_high)
+        dev, group = exchange(dev_low, dev_high, group_low, group_high, tables)
         applied, inverse, sums = call(
             bind(products_kernel),
             [flat, flat, (groups, 1, LANES)],
@@ -477,14 +472,9 @@
         sums = lax.all_to_all(sums, "group", 0, 0)
         (sums,) = call(middle_kernel, [(devs, 1, LANES)], sums)
         sums = lax.all_to_all(sums, "dev", 0, 0)
-        outs = pl.pallas_call(
-            final_kernel,
-            out_shape=(jax.ShapeDtypeStruct(flat, jnp.float32),) * 3,
-            in_specs=[pl.BlockSpec(memory_space=pltpu.VMEM)] * 6,
-            out_specs=(pl.BlockSpec(memory_space=pltpu.HBM),) * 3,
-            scratch_shapes=[pltpu.VMEM(flat, jnp.float32)] * 3 + [pltpu.SemaphoreType.DMA((3,))],
-            compiler_params=pltpu.CompilerParams(vmem_limit_bytes=VMEM_BYTES),
-        )(sums, solution, residual, smooth, applied, inverse)
+        outs = call(
+            final_kernel, [flat] * 3, sums, solution, residual, smooth, applied, inverse
+        )
         return tuple(out.reshape(local) for out in outs)
 
     spec = P("group", "dev", None, None)

time: 81.1 us -> 81.6 us (level)
  local copies, waits for them, and re-layouts: 1.66 us -> 2.52 us
    ppermute x4, starting transfers between devices: 29.9 us -> 28.7 us  [both_ways(): after = lax.ppermute(low, axis, [(j, i) for i, j in up])]
    ppermute x4, starting transfers between devices: 6.83 us -> 7.84 us  [both_ways(): before = lax.ppermute(high, axis, up)]
    pallas_call x1 -> x0, Pallas kernels: 0.88 us -> none  [on_device(): pl.pallas_call(final_kernel, out_shape=(jax.ShapeDtypeStruct(flat, jnp.fl...]
    unnamed x12 -> x14, local copies, waits for them, and re-layouts: 1.66 us -> 2.52 us
    pallas_call x7 -> x8, Pallas kernels: 1.72 us -> 2.58 us  [call(): pl.pallas_call(kernel, out_shape=outs, in_specs=[vmem] * len(args), out_s...]
  transfers between devices with their start and end apart: 8 -> 8, of which waited for: 5 -> 4; matrix products, arithmetic and copies ran while one was open for 0% -> 0% of each run, Pallas kernels for 0% -> 0%
where the time goes in v4:
time: 81.6 us; the launch traced here: 81.2 us
  starting transfers between devices  36.5 us (45%)
  blocking collectives  34.8 us (43%)
  waiting for transfers between devices  3.98 us (5%)
  Pallas kernels  2.58 us (3%)
  local copies, waits for them, and re-layouts  2.52 us (3%)
    ppermute x4, starting transfers between devices, both_ways(): after = lax.ppermute(low, axis, [(j, i) for i, j in up])  28.7 us
    all_to_all x1, blocking collectives, on_device(): sums = lax.all_to_all(sums, 'dev', 0, 0)  18.3 us
    all_to_all x1, blocking collectives, on_device(): sums = lax.all_to_all(sums, 'group', 0, 0)  16.5 us
    ppermute x4, starting transfers between devices, both_ways(): before = lax.ppermute(high, axis, up)  7.84 us
    ppermute x4, waiting for transfers between devices, both_ways(): after = lax.ppermute(low, axis, [(j, i) for i, j in up])  3.32 us
    pallas_call x8, Pallas kernels, call(): pl.pallas_call(kernel, out_shape=outs, in_specs=[vmem] * len(args), out_s...  2.58 us
    unnamed x14, local copies, waits for them, and re-layouts  2.52 us
  transfers between devices with their start and end apart: 8, of which 4 were waited for; matrix products, arithmetic and copies ran while one was open for 0% of the time, Pallas kernels for 0%

profile of v4, /device:TPU:1, one launch (start us, length us, event | category | flops | bytes accessed | tf_op | source)
XLA Modules:
  0.0 81.2 jit_solution(2747844486420998328)
XLA Ops:
  0.6 0.0 copy-start.4
  0.6 0.8 %copy-done.4 = f32[1,2,16,512]{3,2,1,0:T(8,128)S(1)} copy-done((f32[1,2,16,512]{3,2,1,0:T(8,128)S(1)}, f32[1,2,16,512]{3,2,1,0:T(8,128)}, u32[]{:S(2)}) %copy-start.4) | copy-done | bytes 65560
  1.5 0.0 copy-start.3
  1.5 0.3 shard_map.85
  1.7 2.8 %collective-permute-start = (f32[32,128]{1,0:T(8,128)S(1)}, f32[32,128]{1,0:T(8,128)S(1)}, u32[]{:S(2)}, u32[]{:S(2)}) collective-permute-start(f32[32,128]{1,0:T(8,128)S(1)} %get-tuple-element.31), channel_id=1, source_target_pairs={{0,64},{64,128},{128,192},{192,256},{256,320},{320,384},{384,448},... | collective-permute-start | bytes 49160 | tf_op jit(solution)/shard_map/ppermute | solution.py:399
  4.5 11.4 %collective-permute-start.1 = (f32[32,128]{1,0:T(8,128)S(1)}, f32[32,128]{1,0:T(8,128)S(1)}, u32[]{:S(2)}, u32[]{:S(2)}) collective-permute-start(f32[32,128]{1,0:T(8,128)S(1)} %get-tuple-element.32), channel_id=1, source_target_pairs={{64,0},{128,64},{192,128},{256,192},{320,256},{384,320},{448,384},... | collective-permute-start | bytes 49160 | tf_op jit(solution)/shard_map/ppermute | solution.py:400
  15.9 0.0 copy-done.3
  15.9 0.0 copy-start
  15.9 0.9 %copy-done = bf16[3,1,2,16,512]{4,3,2,1,0:T(8,128)(2,1)S(1)} copy-done((bf16[3,1,2,16,512]{4,3,2,1,0:T(8,128)(2,1)S(1)}, bf16[3,1,2,16,512]{4,3,2,1,0:T(8,128)(2,1)}, u32[]{:S(2)}) %copy-start) | copy-done | bytes 98328
  16.8 0.0 copy-start.6
  16.8 0.8 copy-done.6
  17.6 0.0 copy-start.1
  17.6 0.3 shard_map.86
  17.9 0.0 collective-permute-done.refs_2_.refs_3_
  17.9 0.0 collective-permute-done.1.refs_3_.refs_4_
  17.9 0.1 shard_map.87
  18.0 1.9 %collective-permute-start.2 = (f32[16,128]{1,0:T(8,128)S(1)}, f32[16,128]{1,0:T(8,128)S(1)}, u32[]{:S(2)}, u32[]{:S(2)}) collective-permute-start(f32[16,128]{1,0:T(8,128)S(1)} %get-tuple-element.34), channel_id=1, source_target_pairs={{0,1},{1,2},{2,3},{3,4},{4,5},{5,6},{6,7},{7,8},{8,9},{9,10},{10,1... | collective-permute-start | bytes 24584 | tf_op jit(solution)/shard_map/ppermute | solution.py:399
  19.9 9.4 %collective-permute-start.3 = (f32[16,128]{1,0:T(8,128)S(1)}, f32[16,128]{1,0:T(8,128)S(1)}, u32[]{:S(2)}, u32[]{:S(2)}) collective-permute-start(f32[16,128]{1,0:T(8,128)S(1)} %get-tuple-element.35), channel_id=1, source_target_pairs={{1,0},{2,1},{3,2},{4,3},{5,4},{6,5},{7,6},{8,7},{9,8},{10,9},{11,1... | collective-permute-start | bytes 24584 | tf_op jit(solution)/shard_map/ppermute | solution.py:400
  29.3 0.0 collective-permute-done.2.refs_1_
  29.3 0.8 collective-permute-done.3.refs_2_
  30.1 0.0 copy-done.1
  30.1 0.7 shard_map.88
  30.8 0.0 copy-start.2
  30.8 1.2 %collective-permute-start.4 = (f32[32,128]{1,0:T(8,128)S(1)}, f32[32,128]{1,0:T(8,128)S(1)}, u32[]{:S(2)}, u32[]{:S(2)}) collective-permute-start(f32[32,128]{1,0:T(8,128)S(1)} %get-tuple-element.42), channel_id=1, source_target_pairs={{0,64},{64,128},{128,192},{192,256},{256,320},{320,384},{384,448},... | collective-permute-start | bytes 49160 | tf_op jit(solution)/shard_map/ppermute | solution.py:399
  32.0 0.7 collective-permute-start.5
  32.7 0.7 collective-permute-done.4.refs_2_.refs_4_
  33.4 1.8 %collective-permute-done.5.refs_3_.refs_5_ = f32[32,128]{1,0:T(8,128)S(1)} collective-permute-done((f32[32,128]{1,0:T(8,128)S(1)}, f32[32,128]{1,0:T(8,128)S(1)}, u32[]{:S(2)}, u32[]{:S(2)}) %collective-permute-start.5) | collective-permute-done | bytes 16416 | tf_op jit(solution)/shard_map/ppermute | solution.py:400
  35.2 0.1 shard_map.89
  35.3 1.9 %collective-permute-start.6 = (f32[16,128]{1,0:T(8,128)S(1)}, f32[16,128]{1,0:T(8,128)S(1)}, u32[]{:S(2)}, u32[]{:S(2)}) collective-permute-start(f32[16,128]{1,0:T(8,128)S(1)} %get-tuple-element.44), channel_id=1, source_target_pairs={{0,1},{1,2},{2,3},{3,4},{4,5},{5,6},{6,7},{7,8},{8,9},{9,10},{10,1... | collective-permute-start | bytes 24584 | tf_op jit(solution)/shard_map/ppermute | solution.py:399
  37.2 7.2 %collective-permute-start.7 = (f32[16,128]{1,0:T(8,128)S(1)}, f32[16,128]{1,0:T(8,128)S(1)}, u32[]{:S(2)}, u32[]{:S(2)}) collective-permute-start(f32[16,128]{1,0:T(8,128)S(1)} %get-tuple-element.45), channel_id=1, source_target_pairs={{1,0},{2,1},{3,2},{4,3},{5,4},{6,5},{7,6},{8,7},{9,8},{10,9},{11,1... | collective-permute-start | bytes 24584 | tf_op jit(solution)/shard_map/ppermute | solution.py:400
  44.4 0.0 collective-permute-done.6.refs_2_
  44.4 0.8 collective-permute-done.7.refs_3_
  45.2 0.0 copy-done.2
  45.2 0.2 shard_map.90
  45.4 0.0 copy-start.5
  45.4 16.5 %all_to_all.10.parts = f32[16,1,128]{2,1,0:T(1,128)S(1)} all-to-all(f32[16,1,128]{2,1,0:T(1,128)S(1)} %get-tuple-element.47), channel_id=1, replica_groups=mesh['group'=16,'dev'=64] {'group'}, dimensions={0} | all-to-all | bytes 16384 | tf_op jit(solution)/shard_map/all_to_all | solution.py:472
  62.0 18.3 %all_to_all.11.parts = f32[64,1,128]{2,1,0:T(1,128)S(1)} all-to-all(f32[64,1,128]{2,1,0:T(1,128)S(1)} %shard_map.91), channel_id=1, replica_groups=mesh['group'=16,'dev'=64] {'dev'}, dimensions={0} | all-to-all | bytes 65536 | tf_op jit(solution)/shard_map/all_to_all | solution.py:474
  80.3 0.0 copy-done.5
  80.3 0.9 %shard_map.92 = (f32[32,512]{1,0:T(8,128)}, f32[32,512]{1,0:T(8,128)}, f32[32,512]{1,0:T(8,128)}) custom-call(f32[64,1,128]{2,1,0:T(1,128)S(1)} %all_to_all.11.parts, f32[32,512]{1,0:T(8,128)S(1)} %bitcast.15, f32[32,512]{1,0:T(8,128)S(1)} %bitcast.11, f32[32,512]{1,0:T(8,128)S(1)} %get-tuple-element.46.refs_7_.smooth, ...), custom_call_target="tpu_custom_call" | custom-call | tf_op jit(solution)/shard_map/pallas_call | solution.py:387
  (1 shorter events, 0.0 us)
Async XLA Ops:
  0.6 0.8 %copy-start.4 = (f32[1,2,16,512]{3,2,1,0:T(8,128)S(1)}, f32[1,2,16,512]{3,2,1,0:T(8,128)}, u32[]{:S(2)}) copy-start(f32[1,2,16,512]{3,2,1,0:T(8,128)} %param.8) | copy-start | bytes 196612
  1.5 14.4 %copy-start.3 = (bf16[1,2,16,512]{3,2,1,0:T(8,128)(2,1)S(1)}, bf16[1,2,16,512]{3,2,1,0:T(8,128)(2,1)}, u32[]{:S(2)}) copy-start(bf16[1,2,16,512]{3,2,1,0:T(8,128)(2,1)} %param.10) | copy-start | bytes 98308
  1.7 16.2 %collective-permute-start = (f32[32,128]{1,0:T(8,128)S(1)}, f32[32,128]{1,0:T(8,128)S(1)}, u32[]{:S(2)}, u32[]{:S(2)}) collective-permute-start(f32[32,128]{1,0:T(8,128)S(1)} %get-tuple-element.31), channel_id=1, source_target_pairs={{0,64},{64,128},{128,192},{192,256},{256,320},{320,384},{384,448},... | collective-permute-start | bytes 49160 | tf_op jit(solution)/shard_map/ppermute | solution.py:399
  4.5 13.4 %collective-permute-start.1 = (f32[32,128]{1,0:T(8,128)S(1)}, f32[32,128]{1,0:T(8,128)S(1)}, u32[]{:S(2)}, u32[]{:S(2)}) collective-permute-start(f32[32,128]{1,0:T(8,128)S(1)} %get-tuple-element.32), channel_id=1, source_target_pairs={{64,0},{128,64},{192,128},{256,192},{320,256},{384,320},{448,384},... | collective-permute-start | bytes 49160 | tf_op jit(solution)/shard_map/ppermute | solution.py:400
  15.9 0.9 %copy-start = (bf16[3,1,2,16,512]{4,3,2,1,0:T(8,128)(2,1)S(1)}, bf16[3,1,2,16,512]{4,3,2,1,0:T(8,128)(2,1)}, u32[]{:S(2)}) copy-start(bf16[3,1,2,16,512]{4,3,2,1,0:T(8,128)(2,1)} %param.9) | copy-start | bytes 294916
  16.8 0.8 copy-start.6
  17.6 12.5 %copy-start.1 = (bf16[3,1,2,16,512]{4,3,2,1,0:T(8,128)(2,1)S(1)}, bf16[3,1,2,16,512]{4,3,2,1,0:T(8,128)(2,1)}, u32[]{:S(2)}) copy-start(bf16[3,1,2,16,512]{4,3,2,1,0:T(8,128)(2,1)} %param.9) | copy-start | bytes 294916
  18.0 11.3 %collective-permute-start.2 = (f32[16,128]{1,0:T(8,128)S(1)}, f32[16,128]{1,0:T(8,128)S(1)}, u32[]{:S(2)}, u32[]{:S(2)}) collective-permute-start(f32[16,128]{1,0:T(8,128)S(1)} %get-tuple-element.34), channel_id=1, source_target_pairs={{0,1},{1,2},{2,3},{3,4},{4,5},{5,6},{6,7},{7,8},{8,9},{9,10},{10,1... | collective-permute-start | bytes 24584 | tf_op jit(solution)/shard_map/ppermute | solution.py:399
  19.9 10.2 %collective-permute-start.3 = (f32[16,128]{1,0:T(8,128)S(1)}, f32[16,128]{1,0:T(8,128)S(1)}, u32[]{:S(2)}, u32[]{:S(2)}) collective-permute-start(f32[16,128]{1,0:T(8,128)S(1)} %get-tuple-element.35), channel_id=1, source_target_pairs={{1,0},{2,1},{3,2},{4,3},{5,4},{6,5},{7,6},{8,7},{9,8},{10,9},{11,1... | collective-permute-start | bytes 24584 | tf_op jit(solution)/shard_map/ppermute | solution.py:400
  30.8 14.4 %copy-start.2 = (f32[1,2,16,512]{3,2,1,0:T(8,128)S(1)}, f32[1,2,16,512]{3,2,1,0:T(8,128)}, u32[]{:S(2)}) copy-start(f32[1,2,16,512]{3,2,1,0:T(8,128)} %param.7) | copy-start | bytes 196612
  30.8 2.6 %collective-permute-start.4 = (f32[32,128]{1,0:T(8,128)S(1)}, f32[32,128]{1,0:T(8,128)S(1)}, u32[]{:S(2)}, u32[]{:S(2)}) collective-permute-start(f32[32,128]{1,0:T(8,128)S(1)} %get-tuple-element.42), channel_id=1, source_target_pairs={{0,64},{64,128},{128,192},{192,256},{256,320},{320,384},{384,448},... | collective-permute-start | bytes 49160 | tf_op jit(solution)/shard_map/ppermute | solution.py:399
  32.0 3.2 %collective-permute-start.5 = (f32[32,128]{1,0:T(8,128)S(1)}, f32[32,128]{1,0:T(8,128)S(1)}, u32[]{:S(2)}, u32[]{:S(2)}) collective-permute-start(f32[32,128]{1,0:T(8,128)S(1)} %get-tuple-element.43), channel_id=1, source_target_pairs={{64,0},{128,64},{192,128},{256,192},{320,256},{384,320},{448,384},... | collective-permute-start | bytes 49160 | tf_op jit(solution)/shard_map/ppermute | solution.py:400
  35.3 9.2 %collective-permute-start.6 = (f32[16,128]{1,0:T(8,128)S(1)}, f32[16,128]{1,0:T(8,128)S(1)}, u32[]{:S(2)}, u32[]{:S(2)}) collective-permute-start(f32[16,128]{1,0:T(8,128)S(1)} %get-tuple-element.44), channel_id=1, source_target_pairs={{0,1},{1,2},{2,3},{3,4},{4,5},{5,6},{6,7},{7,8},{8,9},{9,10},{10,1... | collective-permute-start | bytes 24584 | tf_op jit(solution)/shard_map/ppermute | solution.py:399
  37.2 8.0 %collective-permute-start.7 = (f32[16,128]{1,0:T(8,128)S(1)}, f32[16,128]{1,0:T(8,128)S(1)}, u32[]{:S(2)}, u32[]{:S(2)}) collective-permute-start(f32[16,128]{1,0:T(8,128)S(1)} %get-tuple-element.45), channel_id=1, source_target_pairs={{1,0},{2,1},{3,2},{4,3},{5,4},{6,5},{7,6},{8,7},{9,8},{10,9},{11,1... | collective-permute-start | bytes 24584 | tf_op jit(solution)/shard_map/ppermute | solution.py:400
  45.4 34.9 %copy-start.5 = (f32[1,2,16,512]{3,2,1,0:T(8,128)S(1)}, f32[1,2,16,512]{3,2,1,0:T(8,128)}, u32[]{:S(2)}) copy-start(f32[1,2,16,512]{3,2,1,0:T(8,128)} %param.6) | copy-start | bytes 196612

commit v5 on v4

--- a/solution.py
+++ b/solution.py
@@ -11,7 +11,7 @@
 TILES = NP**3 // LANES
 HALF = NP * NP
 SECOND = 64
-VMEM_BYTES = 8 * 2**20
+ORDERS = ("dev", "group")
 
 lobatto_nodes = [
     -1.0,
@@ -259,7 +259,25 @@
     diag_out[...] = join(local_assemble(blocks_of(local, dims)))
 
 
-def corner_kernel(dims, dev_low, dev_high, before, after, ready, low_out, high_out):
+def corner_kernel(dims, group_low, group_high, before, after, low_out, high_out):
+    eb, ez = dims
+    low_recv = before[...]
+    high_recv = after[...]
+    lane = lanes(ez)
+    j = (lane // NP) % NP
+    for ref, out, upper in ((group_low, low_out, False), (group_high, high_out, True)):
+        shift_low = NP - HALF if upper else 0
+        shift_high = 0 if upper else HALF - NP
+        blocks = [ref[b * ez : (b + 1) * ez, :] for b in range(eb)]
+        low = roll(low_recv, shift_low, 1) if shift_low else low_recv
+        high = roll(high_recv, shift_high, 1) if shift_high else high_recv
+        blocks[0] = blocks[0] + jnp.where(j == 0, low, 0.0)
+        blocks[-1] = blocks[-1] + jnp.where(j == NP - 1, high, 0.0)
+        for b in range(eb):
+            out[b * ez : (b + 1) * ez, :] = blocks[b]
+
+
+def corner_dev_kernel(dims, dev_low, dev_high, before, after, low_out, high_out):
     eb, ez = dims
     i = (lanes(ez) // NP) % NP
     for ref, out, upper in ((dev_low, low_out, False), (dev_high, high_out, True)):
@@ -389,7 +407,7 @@
         out_shape=outs,
         in_specs=[vmem] * len(args),
         out_specs=(vmem,) * len(outs),
-        compiler_params=pltpu.CompilerParams(vmem_limit_bytes=VMEM_BYTES),
+        compiler_params=pltpu.CompilerParams(vmem_limit_bytes=8 * 2**20),
     )(*args)
 
 
@@ -426,11 +444,13 @@
             body.__name__ = kernel.__name__
             return body
 
-        def exchange(dev_low, dev_high, group_low, group_high, ready):
+        def exchange(order, dev_low, dev_high, group_low, group_high):
+            if order == "dev":
+                dev = both_ways(dev_low, dev_high, "dev")
+                faces = call(bind(corner_kernel), [face_group] * 2, group_low, group_high, *dev)
+                return dev, both_ways(*faces, "group")
             group = both_ways(group_low, group_high, "group")
-            faces = call(
-                bind(corner_kernel), [face_dev] * 2, dev_low, dev_high, *group, ready
-            )
+            faces = call(bind(corner_dev_kernel), [face_dev] * 2, dev_low, dev_high, *group)
             return both_ways(*faces, "dev"), group
 
         field, dev_low, dev_high, group_low, group_high = call(
@@ -445,7 +465,7 @@
             mass,
             tables,
         )
-        dev, group = exchange(dev_low, dev_high, group_low, group_high, tables)
+        dev, group = exchange(ORDERS[0], dev_low, dev_high, group_low, group_high)
         smooth, applied, dev_low, dev_high, group_low, group_high = call(
             bind(operator_kernel),
             [flat, flat, face_dev, face_dev, face_group, face_group],
@@ -458,7 +478,7 @@
             *plane,
             diag,
         )
-        dev, group = exchange(dev_low, dev_high, group_low, group_high, tables)
+        dev, group = exchange(ORDERS[1], dev_low, dev_high, group_low, group_high)
         applied, inverse, sums = call(
             bind(products_kernel),
             [flat, flat, (groups, 1, LANES)],

time: 81.6 us -> 81.1 us (level)
  waiting for transfers between devices: 3.98 us -> 6.26 us
  starting transfers between devices: 36.5 us -> 34.6 us
  local copies, waits for them, and re-layouts: 2.52 us -> 1.66 us
    ppermute x4, starting transfers between devices: 28.7 us -> 25.9 us  [both_ways(): after = lax.ppermute(low, axis, [(j, i) for i, j in up])]
    ppermute x4, waiting for transfers between devices: 3.32 us -> 5.58 us  [both_ways(): after = lax.ppermute(low, axis, [(j, i) for i, j in up])]
    ppermute x4, starting transfers between devices: 7.84 us -> 8.71 us  [both_ways(): before = lax.ppermute(high, axis, up)]
    unnamed x14 -> x12, local copies, waits for them, and re-layouts: 2.52 us -> 1.66 us
  transfers between devices with their start and end apart: 8 -> 8, of which waited for: 4 -> 5; matrix products, arithmetic and copies ran while one was open for 0% -> 0% of each run, Pallas kernels for 0% -> 0%
where the time goes in v5:
time: 81.1 us; the launch traced here: 80.6 us
  blocking collectives  34.8 us (43%)
  starting transfers between devices  34.6 us (43%)
  waiting for transfers between devices  6.26 us (8%)
  Pallas kernels  2.57 us (3%)
  local copies, waits for them, and re-layouts  1.66 us (2%)
    ppermute x4, starting transfers between devices, both_ways(): after = lax.ppermute(low, axis, [(j, i) for i, j in up])  25.9 us
    all_to_all x1, blocking collectives, on_device(): sums = lax.all_to_all(sums, 'dev', 0, 0)  18.3 us
    all_to_all x1, blocking collectives, on_device(): sums = lax.all_to_all(sums, 'group', 0, 0)  16.5 us
    ppermute x4, starting transfers between devices, both_ways(): before = lax.ppermute(high, axis, up)  8.71 us
    ppermute x4, waiting for transfers between devices, both_ways(): after = lax.ppermute(low, axis, [(j, i) for i, j in up])  5.58 us
    pallas_call x8, Pallas kernels, call(): pl.pallas_call(kernel, out_shape=outs, in_specs=[vmem] * len(args), out_s...  2.57 us
    unnamed x12, local copies, waits for them, and re-layouts  1.66 us
  transfers between devices with their start and end apart: 8, of which 5 were waited for; matrix products, arithmetic and copies ran while one was open for 0% of the time, Pallas kernels for 0%

profile of v5, /device:TPU:1, one launch (start us, length us, event | category | flops | bytes accessed | tf_op | source)
XLA Modules:
  0.0 80.6 jit_solution(8259976316574475209)
XLA Ops:
  0.6 0.0 copy-start
  0.6 0.0 copy-start.3
  0.7 0.9 %copy-done.3 = f32[1,2,16,512]{3,2,1,0:T(8,128)S(1)} copy-done((f32[1,2,16,512]{3,2,1,0:T(8,128)S(1)}, f32[1,2,16,512]{3,2,1,0:T(8,128)}, u32[]{:S(2)}) %copy-start.3) | copy-done | bytes 65560
  1.5 0.3 shard_map.85
  1.8 0.0 copy-start.2
  1.8 3.9 %collective-permute-start = (f32[16,128]{1,0:T(8,128)S(1)}, f32[16,128]{1,0:T(8,128)S(1)}, u32[]{:S(2)}, u32[]{:S(2)}) collective-permute-start(f32[16,128]{1,0:T(8,128)S(1)} %get-tuple-element.29), channel_id=1, source_target_pairs={{0,1},{1,2},{2,3},{3,4},{4,5},{5,6},{6,7},{7,8},{8,9},{9,10},{10,1... | collective-permute-start | bytes 24584 | tf_op jit(solution)/shard_map/ppermute | solution.py:417
  5.7 18.1 %collective-permute-start.1 = (f32[16,128]{1,0:T(8,128)S(1)}, f32[16,128]{1,0:T(8,128)S(1)}, u32[]{:S(2)}, u32[]{:S(2)}) collective-permute-start(f32[16,128]{1,0:T(8,128)S(1)} %get-tuple-element.30), channel_id=1, source_target_pairs={{1,0},{2,1},{3,2},{4,3},{5,4},{6,5},{7,6},{8,7},{9,8},{10,9},{11,1... | collective-permute-start | bytes 24584 | tf_op jit(solution)/shard_map/ppermute | solution.py:418
  23.9 0.0 collective-permute-done.refs_2_.refs_1_
  23.9 0.8 collective-permute-done.1.refs_3_.refs_2_
  24.7 0.1 shard_map.86
  24.7 2.8 %collective-permute-start.2 = (f32[32,128]{1,0:T(8,128)S(1)}, f32[32,128]{1,0:T(8,128)S(1)}, u32[]{:S(2)}, u32[]{:S(2)}) collective-permute-start(f32[32,128]{1,0:T(8,128)S(1)} %get-tuple-element.33), channel_id=1, source_target_pairs={{0,64},{64,128},{128,192},{192,256},{256,320},{320,384},{384,448},... | collective-permute-start | bytes 49160 | tf_op jit(solution)/shard_map/ppermute | solution.py:417
  27.6 0.0 collective-permute-start.3
  27.6 0.0 copy-done
  27.6 0.0 copy-done.2
  27.6 0.0 copy-start.5
  27.6 0.8 copy-done.5
  28.4 0.3 shard_map.87
  28.7 0.0 collective-permute-done.2.refs_3_
  28.7 2.0 %collective-permute-done.3.refs_4_ = f32[32,128]{1,0:T(8,128)S(1)} collective-permute-done((f32[32,128]{1,0:T(8,128)S(1)}, f32[32,128]{1,0:T(8,128)S(1)}, u32[]{:S(2)}, u32[]{:S(2)}) %collective-permute-start.3) | collective-permute-done | bytes 16416 | tf_op jit(solution)/shard_map/ppermute | solution.py:418
  30.7 0.7 shard_map.88
  31.4 0.0 copy-start.1
  31.4 0.0 collective-permute-start.4
  31.5 0.5 collective-permute-start.5
  32.0 0.7 collective-permute-done.4.refs_2_.refs_4_
  32.6 2.0 %collective-permute-done.5.refs_3_.refs_5_ = f32[32,128]{1,0:T(8,128)S(1)} collective-permute-done((f32[32,128]{1,0:T(8,128)S(1)}, f32[32,128]{1,0:T(8,128)S(1)}, u32[]{:S(2)}, u32[]{:S(2)}) %collective-permute-start.5) | collective-permute-done | bytes 16416 | tf_op jit(solution)/shard_map/ppermute | solution.py:418
  34.7 0.1 shard_map.89
  34.8 1.9 %collective-permute-start.6 = (f32[16,128]{1,0:T(8,128)S(1)}, f32[16,128]{1,0:T(8,128)S(1)}, u32[]{:S(2)}, u32[]{:S(2)}) collective-permute-start(f32[16,128]{1,0:T(8,128)S(1)} %get-tuple-element.44), channel_id=1, source_target_pairs={{0,1},{1,2},{2,3},{3,4},{4,5},{5,6},{6,7},{7,8},{8,9},{9,10},{10,1... | collective-permute-start | bytes 24584 | tf_op jit(solution)/shard_map/ppermute | solution.py:417
  36.7 7.2 %collective-permute-start.7 = (f32[16,128]{1,0:T(8,128)S(1)}, f32[16,128]{1,0:T(8,128)S(1)}, u32[]{:S(2)}, u32[]{:S(2)}) collective-permute-start(f32[16,128]{1,0:T(8,128)S(1)} %get-tuple-element.45), channel_id=1, source_target_pairs={{1,0},{2,1},{3,2},{4,3},{5,4},{6,5},{7,6},{8,7},{9,8},{10,9},{11,1... | collective-permute-start | bytes 24584 | tf_op jit(solution)/shard_map/ppermute | solution.py:418
  43.9 0.0 collective-permute-done.6.refs_2_
  43.9 0.8 collective-permute-done.7.refs_3_
  44.7 0.0 copy-done.1
  44.7 0.2 shard_map.90
  44.9 0.0 copy-start.4
  44.9 16.5 %all_to_all.10.parts = f32[16,1,128]{2,1,0:T(1,128)S(1)} all-to-all(f32[16,1,128]{2,1,0:T(1,128)S(1)} %get-tuple-element.47), channel_id=1, replica_groups=mesh['group'=16,'dev'=64] {'group'}, dimensions={0} | all-to-all | bytes 16384 | tf_op jit(solution)/shard_map/all_to_all | solution.py:492
  61.5 18.3 %all_to_all.11.parts = f32[64,1,128]{2,1,0:T(1,128)S(1)} all-to-all(f32[64,1,128]{2,1,0:T(1,128)S(1)} %shard_map.91), channel_id=1, replica_groups=mesh['group'=16,'dev'=64] {'dev'}, dimensions={0} | all-to-all | bytes 65536 | tf_op jit(solution)/shard_map/all_to_all | solution.py:494
  79.7 0.0 copy-done.4
  79.7 0.9 %shard_map.92 = (f32[32,512]{1,0:T(8,128)}, f32[32,512]{1,0:T(8,128)}, f32[32,512]{1,0:T(8,128)}) custom-call(f32[64,1,128]{2,1,0:T(1,128)S(1)} %all_to_all.11.parts, f32[32,512]{1,0:T(8,128)S(1)} %bitcast.15, f32[32,512]{1,0:T(8,128)S(1)} %bitcast.11, f32[32,512]{1,0:T(8,128)S(1)} %get-tuple-element.46.refs_7_.smooth, ...), custom_call_target="tpu_custom_call" | custom-call | tf_op jit(solution)/shard_map/pallas_call | solution.py:405
  (1 shorter events, 0.0 us)
Async XLA Ops:
  0.6 26.9 %copy-start = (bf16[3,1,2,16,512]{4,3,2,1,0:T(8,128)(2,1)S(1)}, bf16[3,1,2,16,512]{4,3,2,1,0:T(8,128)(2,1)}, u32[]{:S(2)}) copy-start(bf16[3,1,2,16,512]{4,3,2,1,0:T(8,128)(2,1)} %param.9) | copy-start | bytes 294916
  0.6 0.9 %copy-start.3 = (f32[1,2,16,512]{3,2,1,0:T(8,128)S(1)}, f32[1,2,16,512]{3,2,1,0:T(8,128)}, u32[]{:S(2)}) copy-start(f32[1,2,16,512]{3,2,1,0:T(8,128)} %param.8) | copy-start | bytes 196612
  1.8 25.8 %copy-start.2 = (bf16[1,2,16,512]{3,2,1,0:T(8,128)(2,1)S(1)}, bf16[1,2,16,512]{3,2,1,0:T(8,128)(2,1)}, u32[]{:S(2)}) copy-start(bf16[1,2,16,512]{3,2,1,0:T(8,128)(2,1)} %param.10) | copy-start | bytes 98308
  1.8 22.1 %collective-permute-start = (f32[16,128]{1,0:T(8,128)S(1)}, f32[16,128]{1,0:T(8,128)S(1)}, u32[]{:S(2)}, u32[]{:S(2)}) collective-permute-start(f32[16,128]{1,0:T(8,128)S(1)} %get-tuple-element.29), channel_id=1, source_target_pairs={{0,1},{1,2},{2,3},{3,4},{4,5},{5,6},{6,7},{7,8},{8,9},{9,10},{10,1... | collective-permute-start | bytes 24584 | tf_op jit(solution)/shard_map/ppermute | solution.py:417
  5.7 18.9 %collective-permute-start.1 = (f32[16,128]{1,0:T(8,128)S(1)}, f32[16,128]{1,0:T(8,128)S(1)}, u32[]{:S(2)}, u32[]{:S(2)}) collective-permute-start(f32[16,128]{1,0:T(8,128)S(1)} %get-tuple-element.30), channel_id=1, source_target_pairs={{1,0},{2,1},{3,2},{4,3},{5,4},{6,5},{7,6},{8,7},{9,8},{10,9},{11,1... | collective-permute-start | bytes 24584 | tf_op jit(solution)/shard_map/ppermute | solution.py:418
  24.7 4.0 %collective-permute-start.2 = (f32[32,128]{1,0:T(8,128)S(1)}, f32[32,128]{1,0:T(8,128)S(1)}, u32[]{:S(2)}, u32[]{:S(2)}) collective-permute-start(f32[32,128]{1,0:T(8,128)S(1)} %get-tuple-element.33), channel_id=1, source_target_pairs={{0,64},{64,128},{128,192},{192,256},{256,320},{320,384},{384,448},... | collective-permute-start | bytes 49160 | tf_op jit(solution)/shard_map/ppermute | solution.py:417
  27.6 3.2 %collective-permute-start.3 = (f32[32,128]{1,0:T(8,128)S(1)}, f32[32,128]{1,0:T(8,128)S(1)}, u32[]{:S(2)}, u32[]{:S(2)}) collective-permute-start(f32[32,128]{1,0:T(8,128)S(1)} %get-tuple-element.34), channel_id=1, source_target_pairs={{64,0},{128,64},{192,128},{256,192},{320,256},{384,320},{448,384},... | collective-permute-start | bytes 49160 | tf_op jit(solution)/shard_map/ppermute | solution.py:418
  27.6 0.8 copy-start.5
  31.4 13.3 %copy-start.1 = (f32[1,2,16,512]{3,2,1,0:T(8,128)S(1)}, f32[1,2,16,512]{3,2,1,0:T(8,128)}, u32[]{:S(2)}) copy-start(f32[1,2,16,512]{3,2,1,0:T(8,128)} %param.7) | copy-start | bytes 196612
  31.4 1.2 %collective-permute-start.4 = (f32[32,128]{1,0:T(8,128)S(1)}, f32[32,128]{1,0:T(8,128)S(1)}, u32[]{:S(2)}, u32[]{:S(2)}) collective-permute-start(f32[32,128]{1,0:T(8,128)S(1)} %get-tuple-element.42), channel_id=1, source_target_pairs={{0,64},{64,128},{128,192},{192,256},{256,320},{320,384},{384,448},... | collective-permute-start | bytes 49160 | tf_op jit(solution)/shard_map/ppermute | solution.py:417
  31.5 3.2 %collective-permute-start.5 = (f32[32,128]{1,0:T(8,128)S(1)}, f32[32,128]{1,0:T(8,128)S(1)}, u32[]{:S(2)}, u32[]{:S(2)}) collective-permute-start(f32[32,128]{1,0:T(8,128)S(1)} %get-tuple-element.43), channel_id=1, source_target_pairs={{64,0},{128,64},{192,128},{256,192},{320,256},{384,320},{448,384},... | collective-permute-start | bytes 49160 | tf_op jit(solution)/shard_map/ppermute | solution.py:418
  34.8 9.2 %collective-permute-start.6 = (f32[16,128]{1,0:T(8,128)S(1)}, f32[16,128]{1,0:T(8,128)S(1)}, u32[]{:S(2)}, u32[]{:S(2)}) collective-permute-start(f32[16,128]{1,0:T(8,128)S(1)} %get-tuple-element.44), channel_id=1, source_target_pairs={{0,1},{1,2},{2,3},{3,4},{4,5},{5,6},{6,7},{7,8},{8,9},{9,10},{10,1... | collective-permute-start | bytes 24584 | tf_op jit(solution)/shard_map/ppermute | solution.py:417
  36.7 8.0 %collective-permute-start.7 = (f32[16,128]{1,0:T(8,128)S(1)}, f32[16,128]{1,0:T(8,128)S(1)}, u32[]{:S(2)}, u32[]{:S(2)}) collective-permute-start(f32[16,128]{1,0:T(8,128)S(1)} %get-tuple-element.45), channel_id=1, source_target_pairs={{1,0},{2,1},{3,2},{4,3},{5,4},{6,5},{7,6},{8,7},{9,8},{10,9},{11,1... | collective-permute-start | bytes 24584 | tf_op jit(solution)/shard_map/ppermute | solution.py:418
  44.9 34.8 %copy-start.4 = (f32[1,2,16,512]{3,2,1,0:T(8,128)S(1)}, f32[1,2,16,512]{3,2,1,0:T(8,128)}, u32[]{:S(2)}) copy-start(f32[1,2,16,512]{3,2,1,0:T(8,128)} %param.6) | copy-start | bytes 196612
